TPU v7x, 128 devices: a whole 4x4x4 slice. The times are simulated.
128 devices in a mesh: gx: 32 (over z_lo, y, x), wa: 4 (over z_hi, core).
Axes of the slice: x: 4, y: 4, z: 4 (z_hi: 2, z_lo: 2; z = z_hi * 2 + z_lo), core: 2. Of those that a mesh axis runs over, the one named last changes fastest.
Arguments:
- warm_field: float32 [64, 2, 512, 2048], P('wa', None, 'gx'), may hold values from -1.8 to 1.8
- warm_adjoint: float32 [64, 2, 512, 2048], P('wa', None, 'gx'), may hold values from -1.8 to 1.8
- permittivity: float32 [512, 2048], P('gx'), may hold values from 1 to 12
- design_mask: int32 [512, 2048], P('gx'), may hold values 0 or 1
- source_row: int32 [64], P('wa'), may hold values from 0 to 511
- monitor_row: int32 [64], P('wa'), may hold values from 0 to 511
- wavenumber: float32 [64], P('wa'), may hold values from 0.02 to 0.08
- bloch_phase: float32 [64], P('wa'), may hold values from -3.140625 to 3.140625
- source_profile: float32 [64, 2, 2048], P('wa'), may hold values from -24 to 24
- monitor_profile: float32 [64, 2, 2048], P('wa'), may hold values from -4 to 4
Outputs:
- forward_field: float32 [64, 2, 512, 2048], P('wa', None, 'gx')
- adjoint_field: float32 [64, 2, 512, 2048], P('wa', None, 'gx')
- gradient: float32 [512, 2048], P('gx')
All inputs are finite; a program needn't handle non-finite values. No bound on the sum of `design_mask` on one device may be relied on, other than what follows from the above.
Results may differ from a plain program's by a relative error of at most 0.0003.
Values sent between devices are 32-bit elements; how exact they have to be, the bound alone decides.
No kernel may reach another device: no remote copies, remote signals or barrier semaphores. Data moves between devices by JAX's collectives and lax.ppermute only.
A program may use at most 128 MiB of HBM per device.

v0:
```python
import functools

import jax
import jax.numpy as jnp
from jax import lax
from jax.experimental import pallas as pl
from jax.experimental.pallas import tpu as pltpu
from jax.sharding import PartitionSpec as P

floor_share = 0.5
LANES = 128
SUBLANES = 8
HALO = 3
EPS_ROWS = 2
BASE_SUMS = 9
MARK_SUMS = 6
LINE_SUMS = 27
FWD_SUMS = BASE_SUMS + MARK_SUMS
GROUP_LANES = 64
TABLE_COLUMNS = 7
INNER_LIMIT = 6 * 2**20
OUTER_LIMIT = 4 * 2**20
FINISH_LIMIT = 4 * 2**20
VMEM = pl.BlockSpec(memory_space=pltpu.VMEM)
SMEM = pl.BlockSpec(memory_space=pltpu.SMEM)
HBM = pl.BlockSpec(memory_space=pltpu.HBM)


def lane_slice(j):
    return slice(j * LANES, (j + 1) * LANES)


def is_odd(first_row_ref, rows):
    return lax.rem(first_row_ref[0], 2 * rows) != 0


def pack_kernel(first_row_ref, field_hbm, *refs, with_eps):
    if with_eps:
        eps_ref, first_ref, second_ref, stage_ref, sems = refs
    else:
        first_ref, second_ref, stage_ref, sems = refs
    waves, parts, rows, width = field_hbm.shape
    odd = is_odd(first_row_ref, rows)
    chunks = sems.shape[0]
    span = width // chunks
    loads = []
    for n in range(chunks):
        lanes = pl.ds(n * span, span)
        loads.append(
            pltpu.make_async_copy(
                field_hbm.at[:, :, :, lanes], stage_ref.at[:, :, :, lanes], sems.at[n]
            )
        )
        loads[-1].start()
    if with_eps:
        at = HALO * parts * waves
        low = jnp.tile(eps_ref[:EPS_ROWS, :], (SUBLANES // EPS_ROWS, 1))
        high = jnp.tile(eps_ref[rows - EPS_ROWS :, :], (SUBLANES // EPS_ROWS, 1))
        first_ref[at : at + SUBLANES, :] = jnp.where(odd, low, high)
        second_ref[at : at + SUBLANES, :] = jnp.where(odd, high, low)
    for n in range(chunks):
        loads[n].wait()
        for part in range(parts):
            for wave0 in range(0, waves, SUBLANES):
                for lane0 in range(n * span, (n + 1) * span, LANES):
                    lanes = slice(lane0, lane0 + LANES)
                    group = slice(wave0, wave0 + SUBLANES)
                    head = jnp.swapaxes(stage_ref[group, part, :SUBLANES, lanes], 0, 1)
                    tail = jnp.swapaxes(stage_ref[group, part, rows - SUBLANES :, lanes], 0, 1)
                    for k in range(HALO):
                        at = (k * parts + part) * waves + wave0
                        low = head[k]
                        high = tail[SUBLANES - HALO + k]
                        first_ref[at : at + SUBLANES, lanes] = jnp.where(odd, low, high)
                        second_ref[at : at + SUBLANES, lanes] = jnp.where(odd, high, low)


def outer_rows(first_row, field, eps=None):
    waves, parts, rows, width = field.shape
    height = HALO * parts * waves + (0 if eps is None else SUBLANES)
    shape = jax.ShapeDtypeStruct((height, width), jnp.float32)
    return pl.pallas_call(
        functools.partial(pack_kernel, with_eps=eps is not None),
        in_specs=[SMEM, HBM] + ([] if eps is None else [VMEM]),
        out_specs=[VMEM, VMEM],
        out_shape=[shape, shape],
        scratch_shapes=[
            pltpu.VMEM(field.shape, jnp.float32),
            pltpu.SemaphoreType.DMA((8,)),
        ],
        compiler_params=pltpu.CompilerParams(vmem_limit_bytes=INNER_LIMIT),
        name="outer_rows",
    )(first_row, field, *(() if eps is None else (eps,)))


def lane_neighbours(load, count):
    lane = lax.broadcasted_iota(jnp.int32, (SUBLANES, LANES), 1)
    at_low = lane == 0
    at_high = lane == LANES - 1
    zero = jnp.zeros((SUBLANES, LANES), jnp.float32)
    tile = load(0)
    up_before = zero
    down_here = pltpu.roll(tile, LANES - 1, 1)
    for j in range(count):
        up_here = pltpu.roll(tile, 1, 1)
        if j + 1 < count:
            following = load(j + 1)
            down_after = pltpu.roll(following, LANES - 1, 1)
        else:
            following, down_after = None, zero
        yield (
            j,
            tile,
            jnp.where(at_low, up_before, up_here) + jnp.where(at_high, down_after, down_here),
        )
        tile, up_before, down_here = following, up_here, down_after


class Rows:
    def __init__(self, x_ref, z_ref, u_ref, diag_ref, inv_ref, wave_ref):
        self.x, self.z, self.u = x_ref, z_ref, u_ref
        self.diag, self.inv, self.wave = diag_ref, inv_ref, wave_ref
        _, self.parts, self.waves, width = x_ref.shape
        self.rows = x_ref.shape[0] - 2 * HALO
        self.tiles = width // LANES

    def groups(self):
        return [slice(w, w + SUBLANES) for w in range(0, self.waves, SUBLANES)]

    def column(self, index, group):
        return self.wave[index, group, :]

    def set_diagonal(self, i, eps_row):
        for group in self.groups():
            squared_k = self.column(0, group)
            for j in range(self.tiles):
                lanes = lane_slice(j)
                diagonal = 4.0 - squared_k * jnp.broadcast_to(eps_row(lanes), (SUBLANES, LANES))
                self.diag[i, group, lanes] = diagonal
                self.inv[i, group, lanes] = 1.0 / diagonal

    def residual(self, i):
        for group in self.groups():
            both = [
                lane_neighbours(
                    lambda j, part=part: self.x[i + 1, part, group, lane_slice(j)], self.tiles
                )
                for part in range(self.parts)
            ]
            for steps in zip(*both):
                for part, (j, centre, sides) in enumerate(steps):
                    lanes = lane_slice(j)
                    around = self.x[i, part, group, lanes] + self.x[i + 2, part, group, lanes]
                    self.z[i, part, group, lanes] = (
                        around + sides - self.diag[i, group, lanes] * centre
                    ) * self.inv[i, group, lanes]

    def image(self, i):
        for group in self.groups():
            both = [
                lane_neighbours(
                    lambda j, part=part: self.z[i + 1, part, group, lane_slice(j)], self.tiles
                )
                for part in range(self.parts)
            ]
            for steps in zip(*both):
                for part, (j, centre, sides) in enumerate(steps):
                    lanes = lane_slice(j)
                    around = self.z[i, part, group, lanes] + self.z[i + 2, part, group, lanes]
                    image = self.diag[i + 1, group, lanes] * centre - (around + sides)
                    self.u[i, part, group, lanes] = image * self.inv[i + 1, group, lanes]

    def vectors(self, i, group):
        both = [
            lane_neighbours(
                lambda j, part=part: self.u[i + 1, part, group, lane_slice(j)], self.tiles
            )
            for part in range(self.parts)
        ]
        for steps in zip(*both):
            lanes = lane_slice(steps[0][0])
            diagonal = self.diag[i + 2, group, lanes]
            r, v, w = [], [], []
            for part, (_, centre, sides) in enumerate(steps):
                r.append(diagonal * self.z[i + 2, part, group, lanes])
                v.append(diagonal * centre)
                around = self.u[i, part, group, lanes] + self.u[i + 2, part, group, lanes]
                w.append(v[-1] - (around + sides))
            yield steps[0][0], r, v, w

    def twice(self, i, group, sums):
        rr, rv_re, rv_im, vv, wr_re, wr_im, wv_re, wv_im, ww = sums
        for _, r, v, w in self.vectors(i, group):
            rr += r[0] * r[0] + r[1] * r[1]
            rv_re += r[0] * v[0] + r[1] * v[1]
            rv_im += r[0] * v[1] - r[1] * v[0]
            vv += v[0] * v[0] + v[1] * v[1]
            wr_re += w[0] * r[0] + w[1] * r[1]
            wr_im += w[0] * r[1] - w[1] * r[0]
            wv_re += w[0] * v[0] + w[1] * v[1]
            wv_im += w[0] * v[1] - w[1] * v[0]
            ww += w[0] * w[0] + w[1] * w[1]
        return rr, rv_re, rv_im, vv, wr_re, wr_im, wv_re, wv_im, ww

    def any_at(self, table_ref, row):
        hit = table_ref[0] == row
        for w in range(1, self.waves):
            hit = jnp.logical_or(hit, table_ref[w] == row)
        return hit

    def source(self, i, first_row, total_rows, side_row_ref, side_ref):
        row = first_row + i - 2
        row = jnp.where(row < 0, row + total_rows, row)
        row = jnp.where(row >= total_rows, row - total_rows, row)

        @pl.when(self.any_at(side_row_ref, row))
        def _():
            for group in self.groups():
                cosine, sine = self.frame(i - 2, group)
                chosen = self.column(5, group) == row.astype(jnp.float32)
                for j in range(self.tiles):
                    lanes = lane_slice(j)
                    re = side_ref[group, 0, lanes]
                    im = side_ref[group, 1, lanes]
                    inverse = self.inv[i, group, lanes]
                    self.z[i, 0, group, lanes] += jnp.where(
                        chosen, (cosine * re - sine * im) * inverse, 0.0
                    )
                    self.z[i, 1, group, lanes] += jnp.where(
                        chosen, (sine * re + cosine * im) * inverse, 0.0
                    )

    def frame(self, row, group):
        below = row < 0
        above = row >= self.rows
        return (
            jnp.where(below, self.column(1, group), jnp.where(above, self.column(3, group), 1.0)),
            jnp.where(below, self.column(2, group), jnp.where(above, self.column(4, group), 0.0)),
        )


def wave_column(ref, wave0):
    sublane = lax.broadcasted_iota(jnp.int32, (SUBLANES, LANES), 0)
    out = jnp.zeros((SUBLANES, LANES), jnp.float32)
    for k in range(SUBLANES):
        out = jnp.where(sublane == k, ref[wave0 + k].astype(jnp.float32), out)
    return out


def fill_table(table_ref, wave_refs, first_row, rows, total_rows, sign):
    squared_k_ref, cosine_ref, sine_ref, source_ref, monitor_ref = wave_refs
    at_first = first_row == 0
    at_last = first_row == total_rows - rows
    for wave0 in range(0, table_ref.shape[1], SUBLANES):
        group = slice(wave0, wave0 + SUBLANES)
        cosine = wave_column(cosine_ref, wave0)
        sine = sign * wave_column(sine_ref, wave0)
        table_ref[0, group, :] = wave_column(squared_k_ref, wave0)
        table_ref[1, group, :] = jnp.where(at_first, cosine, 1.0)
        table_ref[2, group, :] = jnp.where(at_first, -sine, 0.0)
        table_ref[3, group, :] = jnp.where(at_last, cosine, 1.0)
        table_ref[4, group, :] = jnp.where(at_last, sine, 0.0)
        table_ref[5, group, :] = wave_column(source_ref, wave0)
        table_ref[6, group, :] = wave_column(monitor_ref, wave0)


def lanes_of(out, totals, wave0, offset):
    lane = lax.broadcasted_iota(jnp.int32, (SUBLANES, LANES), 1)
    base = wave0 // SUBLANES * GROUP_LANES + offset
    for n, total in enumerate(totals):
        out = jnp.where(lane == base + n, jnp.sum(total, axis=1, keepdims=True), out)
    return out


def inner_kernel(*refs, forward, total_rows):
    first_row_ref, *wave_refs = refs[:6]
    field_hbm, refs = refs[6], refs[7:]
    side_row_ref = wave_refs[3]
    if forward:
        (eps_ref, side_ref) = refs[:2]
        (x_ref, z_ref, u_ref, sums_ref, diag_ref, inv_ref, stage_ref, table_ref, sems) = refs[2:]
    else:
        (diag_ref, inv_ref) = refs[:2]
        (x_ref, z_ref, u_ref, sums_ref, stage_ref, table_ref, sems) = refs[2:]
    step = Rows(x_ref, z_ref, u_ref, diag_ref, inv_ref, table_ref)
    rows, waves = step.rows, step.waves
    chunks = sems.shape[0]
    span = step.tiles * LANES // chunks
    loads = []
    for n in range(chunks):
        lanes = pl.ds(n * span, span)
        loads.append(
            pltpu.make_async_copy(
                field_hbm.at[:, :, :, lanes], stage_ref.at[:, :, :, lanes], sems.at[n]
            )
        )
        loads[-1].start()
    fill_table(
        table_ref, wave_refs, first_row_ref[0], rows, total_rows, 1.0 if forward else -1.0
    )
    if forward:
        for row in range(rows):
            step.set_diagonal(row + 2, lambda lanes, row=row: eps_ref[row : row + 1, lanes])
    for n in range(chunks):
        loads[n].wait()
        for part in range(step.parts):
            for group in step.groups():
                for row0 in range(0, rows, SUBLANES):
                    for lane0 in range(n * span, (n + 1) * span, LANES):
                        lanes = slice(lane0, lane0 + LANES)
                        x_ref[HALO + row0 : HALO + row0 + SUBLANES, part, group, lanes] = (
                            jnp.swapaxes(
                                stage_ref[group, part, row0 : row0 + SUBLANES, lanes], 0, 1
                            )
                        )

    def residual(i, _):
        step.residual(i)
        if forward:
            step.source(i, first_row_ref[0], total_rows, side_row_ref, side_ref)
        return 0

    def image(i, _):
        step.image(i)
        return 0

    lax.fori_loop(3, rows + 1, residual, 0)
    lax.fori_loop(3, rows - 1, image, 0)
    zero = jnp.zeros((SUBLANES, LANES), jnp.float32)
    out = zero
    for group in step.groups():
        sums = lax.fori_loop(
            3,
            rows - 3,
            lambda i, sums, group=group: step.twice(i, group, sums),
            (zero,) * BASE_SUMS,
        )
        out = lanes_of(out, sums, group.start, 0 if forward else FWD_SUMS)
    sums_ref[...] = out


def outer_kernel(*refs, forward, total_rows):
    first_row_ref, *wave_refs = refs[:6]
    row_ref, mark_row_ref = wave_refs[3:]
    first_ref, second_ref = refs[6:8]
    if forward:
        (part_ref, _, _, _, _, _, side_ref, mark_ref) = refs[8:16]
        (x_ref, z_ref, u_ref, diag_ref, inv_ref, sums_ref, table_ref, mark_sums) = refs[16:]
    else:
        (part_ref, _, _, _, diag_ref, inv_ref, mark_ref, fwd_sums_ref) = refs[8:16]
        (x_ref, z_ref, u_ref, sums_ref, line_ref, table_ref, line_sums, g_ref) = refs[16:]
    step = Rows(x_ref, z_ref, u_ref, diag_ref, inv_ref, table_ref)
    rows, parts, waves, tiles = step.rows, step.parts, step.waves, step.tiles
    odd = is_odd(first_row_ref, rows)
    first_row = first_row_ref[0]
    fill_table(table_ref, wave_refs, first_row, rows, total_rows, 1.0 if forward else -1.0)
    for group in step.groups():
        for base, offset, swap in ((0, 1, False), (HALO + rows, 3, True)):
            cosine = step.column(offset, group)
            sine = step.column(offset + 1, group)
            for k in range(HALO):
                for j in range(tiles):
                    lanes = lane_slice(j)
                    values = []
                    for part in range(parts):
                        at = (k * parts + part) * waves + group.start
                        one = first_ref[at : at + SUBLANES, lanes]
                        two = second_ref[at : at + SUBLANES, lanes]
                        values.append(jnp.where(odd, two, one) if swap else jnp.where(odd, one, two))
                    re, im = values
                    x_ref[base + k, 0, group, lanes] = cosine * re - sine * im
                    x_ref[base + k, 1, group, lanes] = sine * re + cosine * im
    if forward:
        at = HALO * parts * waves
        for k in range(EPS_ROWS):

            def above_eps(lanes, k=k):
                row = slice(at + k, at + k + 1)
                return jnp.where(odd, first_ref[row, lanes], second_ref[row, lanes])

            def below_eps(lanes, k=k):
                row = slice(at + k, at + k + 1)
                return jnp.where(odd, second_ref[row, lanes], first_ref[row, lanes])

            step.set_diagonal(k, above_eps)
            step.set_diagonal(rows + 2 + k, below_eps)

    def outer(t, count):
        return jnp.where(t < 3, t, t + count - 6)

    def residual(t, _):
        i = outer(t, rows + 4)
        step.residual(i)
        if forward:
            step.source(i, first_row, total_rows, row_ref, side_ref)
        return 0

    def image(t, _):
        step.image(outer(t, rows + 2))
        return 0

    lax.fori_loop(0, 6, residual, 0)
    lax.fori_loop(0, 6, image, 0)
    zero = jnp.zeros((SUBLANES, LANES), jnp.float32)
    base_sums = []
    for group in step.groups():
        base_sums.append(
            lax.fori_loop(
                0,
                6,
                lambda t, sums, group=group: step.twice(outer(t, rows), group, sums),
                (zero,) * BASE_SUMS,
            )
        )
    if forward:
        mark_sums[...] = jnp.zeros_like(mark_sums)

        def mark_at(i, _):
            row = first_row + i

            @pl.when(step.any_at(mark_row_ref, row))
            def _():
                for group in step.groups():
                    chosen = step.column(6, group) == row.astype(jnp.float32)
                    for j in range(tiles):
                        lanes = lane_slice(j)
                        m_re = jnp.where(chosen, mark_ref[group, 0, lanes], 0.0)
                        m_im = jnp.where(chosen, mark_ref[group, 1, lanes], 0.0)
                        for n, (ref, shift) in enumerate(((x_ref, 3), (z_ref, 2), (u_ref, 1))):
                            f_re = ref[i + shift, 0, group, lanes]
                            f_im = ref[i + shift, 1, group, lanes]
                            mark_sums[2 * n, group] += m_re * f_re + m_im * f_im
                            mark_sums[2 * n + 1, group] += m_re * f_im - m_im * f_re

            return 0

        lax.fori_loop(0, rows, mark_at, 0)
        extra, count = mark_sums, MARK_SUMS
    else:
        line_terms(step, first_row, total_rows, mark_row_ref, mark_ref, line_ref, line_sums, g_ref)
        extra, count = line_sums, LINE_SUMS
    out = part_ref[...]
    new = jnp.zeros((SUBLANES, LANES), jnp.float32)
    for n, group in enumerate(step.groups()):
        more = list(base_sums[n]) + [extra[k, group] for k in range(count)]
        new = lanes_of(new, more, group.start, 0 if forward else FWD_SUMS)
    out = out + new
    if forward:
        sums_ref[...] = out
    else:
        out = out + fwd_sums_ref[...]
        for n in range(sums_ref.shape[0]):
            sums_ref[n] = out


def distance_to(row, first_row, total_rows):
    away = row - first_row
    away = jnp.where(away >= total_rows - 2, away - total_rows, away)
    return jnp.where(away < -2, away + total_rows, away)


def dot(a, b):
    return a[0] * b[0] + a[1] * b[1], a[0] * b[1] - a[1] * b[0]


def line_terms(step, first_row, total_rows, mark_row_ref, mark_ref, line_ref, line_sums, g_ref):
    rows, tiles = step.rows, step.tiles
    line_ref[...] = jnp.zeros_like(line_ref)
    line_sums[...] = jnp.zeros_like(line_sums)
    sublane = lax.broadcasted_iota(jnp.int32, (SUBLANES, LANES), 0)

    def one_wave(w, _):
        away = distance_to(mark_row_ref[w], first_row, total_rows)

        @pl.when(away <= rows + 1)
        def _():
            group = pl.ds(pl.multiple_of((w // SUBLANES) * SUBLANES, SUBLANES), SUBLANES)
            mine = sublane == w % SUBLANES
            cosine, sine = step.frame(away, group)
            before = jnp.maximum(away + 1, 0)
            after = jnp.minimum(away + 3, rows + 3)
            for j in range(tiles):
                lanes = lane_slice(j)
                m_re = jnp.where(mine, mark_ref[group, 0, lanes], 0.0)
                m_im = jnp.where(mine, mark_ref[group, 1, lanes], 0.0)
                g = (cosine * m_re + sine * m_im, sine * m_re - cosine * m_im)
                inverse = step.inv[away + 2, group, lanes]
                for part in range(2):
                    z = g[part] * inverse
                    g_ref[0, part, :, lanes] = g[part]
                    g_ref[1, part, :, lanes] = z
                    g_ref[2, part, :, lanes] = -z * step.inv[before, group, lanes]
                    g_ref[4, part, :, lanes] = -z * step.inv[after, group, lanes]
            for part in range(2):
                for j, _, sides in lane_neighbours(
                    lambda j, part=part: g_ref[1, part, :, lane_slice(j)], tiles
                ):
                    lanes = lane_slice(j)
                    image = g_ref[0, part, :, lanes] - sides
                    g_ref[5, part, :, lanes] = image
                    g_ref[3, part, :, lanes] = image * step.inv[away + 2, group, lanes]
            for part in range(2):
                for j in range(tiles):
                    lanes = lane_slice(j)
                    for n in range(4):
                        line_ref[n, part, group, lanes] += g_ref[n + 1, part, :, lanes]
            for k in range(-2, 3):

                @pl.when(jnp.logical_and(away + k >= 0, away + k < rows))
                def _(k=k):
                    zero = jnp.zeros((SUBLANES, LANES), jnp.float32)
                    totals = [zero] * LINE_SUMS

                    def add(at, pair):
                        totals[at] = totals[at] + pair[0]
                        totals[at + 1] = totals[at + 1] + pair[1]

                    if abs(k) < 2:
                        sides_of = [
                            [
                                sides
                                for _, _, sides in lane_neighbours(
                                    lambda j, part=part: g_ref[3 + k, part, :, lane_slice(j)],
                                    tiles,
                                )
                            ]
                            for part in range(2)
                        ]
                    for j, r, v, w_vec in step.vectors(away + k, group):
                        lanes = lane_slice(j)
                        get = lambda n: [g_ref[n, part, :, lanes] for part in range(2)]
                        r = [jnp.where(mine, t, 0.0) for t in r]
                        v = [jnp.where(mine, t, 0.0) for t in v]
                        w_vec = [jnp.where(mine, t, 0.0) for t in w_vec]
                        if abs(k) == 2:
                            wg = [-t for t in get(2 if k < 0 else 4)]
                        elif abs(k) == 1:
                            vg = [-t for t in get(1)]
                            mid = get(3)
                            wg = [vg[p] - mid[p] - sides_of[p][j] for p in range(2)]
                        else:
                            g, vg, low, high = get(0), get(5), get(2), get(4)
                            wg = [
                                vg[p] - (low[p] + high[p]) - sides_of[p][j] for p in range(2)
                            ]
                        add(0, dot(wg, r))
                        add(2, dot(wg, v))
                        add(4, dot(w_vec, wg))
                        totals[6] = totals[6] + dot(wg, wg)[0]
                        if abs(k) < 2:
                            add(7, dot(r, vg))
                            add(9, dot(v, vg))
                            add(11, dot(w_vec, vg))
                            add(13, dot(wg, vg))
                            totals[15] = totals[15] + dot(vg, vg)[0]
                        if k == 0:
                            add(16, dot(r, g))
                            add(18, dot(g, v))
                            add(20, dot(g, vg))
                            add(22, dot(w_vec, g))
                            add(24, dot(wg, g))
                            totals[26] = totals[26] + dot(g, g)[0]
                    used = 7 if abs(k) == 2 else 16 if abs(k) == 1 else LINE_SUMS
                    for n in range(used):
                        line_sums[n, group] += totals[n]

        return 0

    lax.fori_loop(0, step.waves, one_wave, 0)


def array(*shape):
    return jax.ShapeDtypeStruct(shape, jnp.float32)


def inner_rows(forward, field, scalars, extra, total_rows):
    waves, parts, rows, width = field.shape
    args = (*scalars, field, *extra)
    out_shape = [
        array(rows + 6, parts, waves, width),
        array(rows + 4, parts, waves, width),
        array(rows + 2, parts, waves, width),
        array(SUBLANES, LANES),
    ]
    if forward:
        out_shape += [array(rows + 4, waves, width)] * 2
    return pl.pallas_call(
        functools.partial(inner_kernel, forward=forward, total_rows=total_rows),
        in_specs=[SMEM] * 6 + [HBM, VMEM, VMEM],
        out_specs=[VMEM] * len(out_shape),
        out_shape=out_shape,
        scratch_shapes=[
            pltpu.VMEM((waves, parts, rows, width), jnp.float32),
            pltpu.VMEM((TABLE_COLUMNS, waves, LANES), jnp.float32),
            pltpu.SemaphoreType.DMA((4,)),
        ],
        compiler_params=pltpu.CompilerParams(vmem_limit_bytes=INNER_LIMIT),
        name="forward_inner" if forward else "adjoint_inner",
    )(*args)


def outer_rows_solve(forward, scalars, received, inner, more, copies, total_rows):
    x, z, u, sums, diag, inv = inner
    waves = x.shape[2]
    args = (*scalars, *received, sums, x, z, u, diag, inv, *more)
    scratch = [pltpu.VMEM((TABLE_COLUMNS, waves, LANES), jnp.float32)]
    if forward:
        out_shape = [array(*a.shape) for a in (x, z, u, diag, inv, sums)]
        aliases = {9: 0, 10: 1, 11: 2, 12: 3, 13: 4}
        scratch += [pltpu.VMEM((MARK_SUMS, waves, LANES), jnp.float32)]
    else:
        out_shape = [array(*a.shape) for a in (x, z, u)] + [
            array(copies, SUBLANES, LANES),
            array(4, 2, waves, x.shape[-1]),
        ]
        aliases = {9: 0, 10: 1, 11: 2}
        scratch += [
            pltpu.VMEM((LINE_SUMS, waves, LANES), jnp.float32),
            pltpu.VMEM((6, 2, SUBLANES, x.shape[-1]), jnp.float32),
        ]
    return pl.pallas_call(
        functools.partial(outer_kernel, forward=forward, total_rows=total_rows),
        in_specs=[SMEM] * 6 + [VMEM] * (len(args) - 6),
        out_specs=[VMEM] * len(out_shape),
        out_shape=out_shape,
        scratch_shapes=scratch,
        input_output_aliases=aliases,
        compiler_params=pltpu.CompilerParams(vmem_limit_bytes=OUTER_LIMIT),
        name="forward_outer" if forward else "adjoint_outer",
    )(*args)


def finish_kernel(
    first_row_ref,
    squared_k_ref,
    mark_row_ref,
    sums_ref,
    xf_ref,
    zf_ref,
    uf_ref,
    xa_ref,
    _z_in,
    _u_in,
    line_ref,
    fwd_hbm,
    adj_hbm,
    grad_ref,
    za_ref,
    ua_ref,
    coef_ref,
    fwd_stage,
    adj_stage,
    sems,
    *,
    total_rows,
):
    waves, parts, rows, width = fwd_hbm.shape
    tiles = width // LANES
    groups = [slice(w, w + SUBLANES) for w in range(0, waves, SUBLANES)]

    def column(index, group):
        return coef_ref[index, group, :]

    sums = jnp.sum(sums_ref[...], axis=0)
    for group in groups:
        base = group.start // SUBLANES * GROUP_LANES
        cols = [
            jnp.broadcast_to(sums[:, base + n : base + n + 1], (SUBLANES, LANES))
            for n in range(FWD_SUMS + BASE_SUMS + LINE_SUMS)
        ]
        fwd_coefs = step_lengths(*cols[:BASE_SUMS])
        a_re, a_im, b_re, b_im = fwd_coefs
        s0_re, s0_im, s1_re, s1_im, s2_re, s2_im = cols[BASE_SUMS:FWD_SUMS]
        over_re = s0_re + (a_re * s1_re - a_im * s1_im) + (b_re * s2_re - b_im * s2_im)
        over_im = s0_im + (a_re * s1_im + a_im * s1_re) + (b_re * s2_im + b_im * s2_re)
        adj_cols = cols[FWD_SUMS:]
        adj_coefs = step_lengths(
            *with_line(adj_cols[:BASE_SUMS], adj_cols[BASE_SUMS:], over_re, -over_im)
        )
        twice_k = 2.0 * wave_column(squared_k_ref, group.start)
        for n, value in enumerate((*fwd_coefs, *adj_coefs, twice_k, over_re, -over_im)):
            coef_ref[n, group, :] = value

    def one_wave(w, _):
        away = distance_to(mark_row_ref[w], first_row_ref[0], total_rows)

        @pl.when(away <= rows)
        def _():
            group = pl.ds(pl.multiple_of((w // SUBLANES) * SUBLANES, SUBLANES), SUBLANES)
            mine = lax.broadcasted_iota(jnp.int32, (SUBLANES, LANES), 0) == w % SUBLANES
            b_re = jnp.where(mine, column(9, group), 0.0)
            b_im = jnp.where(mine, column(10, group), 0.0)
            for n, (ref, shift, k) in enumerate(
                ((za_ref, 2, 0), (ua_ref, 1, -1), (ua_ref, 1, 0), (ua_ref, 1, 1))
            ):

                @pl.when(jnp.logical_and(away + k >= 0, away + k < rows))
                def _(n=n, ref=ref, at=away + k + shift):
                    for j in range(tiles):
                        lanes = lane_slice(j)
                        re = line_ref[n, 0, group, lanes]
                        im = line_ref[n, 1, group, lanes]
                        ref[at, 0, group, lanes] += b_re * re - b_im * im
                        ref[at, 1, group, lanes] += b_re * im + b_im * re

        return 0

    lax.fori_loop(0, waves, one_wave, 0)
    sublane = lax.broadcasted_iota(jnp.int32, (SUBLANES, LANES), 0)

    def copies(j, slot):
        at = pl.ds(j * LANES, LANES)
        if not isinstance(j, int):
            at = pl.ds(pl.multiple_of(j * LANES, LANES), LANES)
        return [
            pltpu.make_async_copy(fwd_stage.at[slot], fwd_hbm.at[:, :, :, at], sems.at[slot, 0]),
            pltpu.make_async_copy(adj_stage.at[slot], adj_hbm.at[:, :, :, at], sems.at[slot, 1]),
        ]

    def tile_step(j, _):
        slot = lax.rem(j, 2)
        lanes = pl.ds(pl.multiple_of(j * LANES, LANES), LANES)

        @pl.when(j >= 2)
        def _():
            for copy in copies(j - 2, slot):
                copy.wait()

        for row0 in range(0, rows, SUBLANES):
            terms = [jnp.zeros((SUBLANES, LANES), jnp.float32)] * SUBLANES
            for group in groups:
                coefs = [column(n, group) for n in range(9)]
                results = [[], [], [], []]
                for k in range(SUBLANES):
                    row = row0 + k
                    values = []
                    for base, x_ref, z_ref, u_ref in (
                        (0, xf_ref, zf_ref, uf_ref),
                        (4, xa_ref, za_ref, ua_ref),
                    ):
                        a_re, a_im, b_re, b_im = coefs[base : base + 4]
                        z_re = z_ref[row + 2, 0, group, lanes]
                        z_im = z_ref[row + 2, 1, group, lanes]
                        u_re = u_ref[row + 1, 0, group, lanes]
                        u_im = u_ref[row + 1, 1, group, lanes]
                        values.append(
                            x_ref[row + HALO, 0, group, lanes]
                            + (a_re * z_re - a_im * z_im)
                            + (b_re * u_re - b_im * u_im)
                        )
                        values.append(
                            x_ref[row + HALO, 1, group, lanes]
                            + (a_re * z_im + a_im * z_re)
                            + (b_re * u_im + b_im * u_re)
                        )
                    f_re, f_im, g_re, g_im = values
                    terms[k] = terms[k] + coefs[8] * (g_re * f_re - g_im * f_im)
                    for n in range(4):
                        results[n].append(values[n])
                for n, (ref, part) in enumerate(
                    ((fwd_stage, 0), (fwd_stage, 1), (adj_stage, 0), (adj_stage, 1))
                ):
                    ref[slot, group, part, row0 : row0 + SUBLANES, :] = jnp.swapaxes(
                        jnp.stack(results[n]), 0, 1
                    )
            out = jnp.zeros((SUBLANES, LANES), jnp.float32)
            for k in range(SUBLANES):
                out = jnp.where(sublane == k, jnp.sum(terms[k], axis=0, keepdims=True), out)
            grad_ref[row0 : row0 + SUBLANES, lanes] = out
        for copy in copies(j, slot):
            copy.start()
        return 0

    lax.fori_loop(0, tiles, tile_step, 0)
    for j in (tiles - 2, tiles - 1):
        for copy in copies(j, j % 2):
            copy.wait()


def finish(scalars, sums, forward_parts, adjoint_parts, line, total_rows):
    x, z, u = forward_parts
    rows, parts, waves, width = x.shape[0] - 2 * HALO, *x.shape[1:]
    field = array(waves, parts, rows, width)
    stage = pltpu.VMEM((2, waves, parts, rows, LANES), jnp.float32)
    return pl.pallas_call(
        functools.partial(finish_kernel, total_rows=total_rows),
        in_specs=[SMEM] * 3 + [VMEM] * 8,
        out_specs=[HBM, HBM, VMEM, VMEM, VMEM],
        out_shape=[field, field, array(rows, width), array(*z.shape), array(*u.shape)],
        scratch_shapes=[
            pltpu.VMEM((11, waves, LANES), jnp.float32),
            stage,
            stage,
            pltpu.SemaphoreType.DMA((2, 2)),
        ],
        input_output_aliases={8: 3, 9: 4},
        compiler_params=pltpu.CompilerParams(vmem_limit_bytes=FINISH_LIMIT),
        name="finish",
    )(*scalars, sums, *forward_parts, *adjoint_parts, line)[:3]


def step_lengths(rr, rv_re, rv_im, vv, wr_re, wr_im, wv_re, wv_im, ww):
    half = floor_share * rr
    bounded = jnp.maximum(rv_re * rv_re + rv_im * rv_im, half * half)
    a_re = rr * rv_re / bounded
    a_im = -rr * rv_im / bounded
    a_sq = a_re * a_re + a_im * a_im
    ts_re = rv_re - a_re * vv - (a_re * wr_re + a_im * wr_im) + a_sq * wv_re
    ts_im = -rv_im - a_im * vv - (a_re * wr_im - a_im * wr_re) + a_sq * wv_im
    tt = vv - 2.0 * (a_re * wv_re + a_im * wv_im) + a_sq * ww
    o_re = ts_re / tt
    o_im = ts_im / tt
    return (a_re + o_re, a_im + o_im, a_im * o_im - a_re * o_re, -(a_re * o_im + a_im * o_re))


def with_line(base, line, b_re, b_im):
    rr, rv_re, rv_im, vv, wr_re, wr_im, wv_re, wv_im, ww = base
    b_sq = b_re * b_re + b_im * b_im

    def pair(at):
        return line[at], line[at + 1]

    def times(p):
        return b_re * p[0] - b_im * p[1], b_re * p[1] + b_im * p[0]

    def times_conj(p):
        return b_re * p[0] + b_im * p[1], b_re * p[1] - b_im * p[0]

    def mixed(re, im, forth, back, both):
        f, h = times(forth), times_conj(back)
        return re + f[0] + h[0] + b_sq * both[0], im + f[1] + h[1] + b_sq * both[1]

    def square(value, cross, both):
        return value + 2.0 * times(cross)[0] + b_sq * both

    rv_re, rv_im = mixed(rv_re, rv_im, pair(7), pair(18), pair(20))
    wr_re, wr_im = mixed(wr_re, wr_im, pair(22), pair(0), pair(24))
    wv_re, wv_im = mixed(wv_re, wv_im, pair(11), pair(2), pair(13))
    rr = square(rr, pair(16), line[26])
    vv = square(vv, pair(9), line[15])
    ww = square(ww, pair(4), line[6])
    return rr, rv_re, rv_im, vv, wr_re, wr_im, wv_re, wv_im, ww


def local(
    warm_field,
    warm_adjoint,
    permittivity,
    design_mask,
    source_row,
    monitor_row,
    wavenumber,
    bloch_phase,
    source_profile,
    monitor_profile,
):
    rows = permittivity.shape[0]
    count = lax.axis_size("gx")
    index = lax.axis_index("gx")
    total_rows = rows * count
    first_row = (index * rows).astype(jnp.int32).reshape(1)
    pairing_one = [(i, i ^ 1) for i in range(count)]
    pairing_two = [(i, (i + 1 if i % 2 else i - 1) % count) for i in range(count)]
    fwd_first, fwd_second = outer_rows(first_row, warm_field, permittivity)
    fwd_got = (
        lax.ppermute(fwd_first, "gx", pairing_one),
        lax.ppermute(fwd_second, "gx", pairing_two),
    )
    adj_first, adj_second = outer_rows(first_row, warm_adjoint)
    adj_got = (
        lax.ppermute(adj_first, "gx", pairing_one),
        lax.ppermute(adj_second, "gx", pairing_two),
    )
    scalars = (
        first_row,
        wavenumber,
        jnp.cos(bloch_phase),
        jnp.sin(bloch_phase),
        source_row,
        monitor_row,
    )
    fx, fz, fu, f_sums, diag, inv = inner_rows(
        True, warm_field, scalars, (permittivity, source_profile), total_rows
    )
    ax, az, au, a_sums = inner_rows(False, warm_adjoint, scalars, (diag, inv), total_rows)
    fx, fz, fu, diag, inv, f_sums = outer_rows_solve(
        True,
        scalars,
        fwd_got,
        (fx, fz, fu, f_sums, diag, inv),
        (source_profile, monitor_profile),
        count,
        total_rows,
    )
    ax, az, au, sums, line = outer_rows_solve(
        False,
        scalars,
        adj_got,
        (ax, az, au, a_sums, diag, inv),
        (monitor_profile, f_sums),
        count,
        total_rows,
    )
    forward, adjoint, partial = finish(
        (first_row, wavenumber, monitor_row),
        lax.all_to_all(sums, "gx", 0, 0, tiled=True),
        (fx, fz, fu),
        (ax, az, au),
        line,
        total_rows,
    )
    summed_terms = lax.all_gather(partial, "wa").sum(axis=0)
    gradient = design_mask.astype(jnp.float32) * summed_terms
    return (forward, adjoint, gradient)


def solution(mesh):
    placed = (
        P("wa", None, "gx", None),
        P("wa", None, "gx", None),
        P("gx", None),
        P("gx", None),
        P("wa"),
        P("wa"),
        P("wa"),
        P("wa"),
        P("wa", None, None),
        P("wa", None, None),
    )
    return jax.shard_map(
        local,
        mesh=mesh,
        in_specs=placed,
        out_specs=(P("wa", None, "gx", None), P("wa", None, "gx", None), P("gx", None)),
        check_vma=False,
    )
```

profile of v0, /device:TPU:1, one launch (start us, length us, event | category | flops | bytes accessed | tf_op | source)
XLA Modules:
  0.0 93.7 jit_solution(3501473433337209263)
XLA Ops:
  0.6 0.0 copy-start.12
  0.6 0.0 copy-start.10
  0.7 0.0 copy-start.9
  0.7 0.0 copy-start.8
  0.7 0.0 copy-start
  0.7 2.2 %copy-done = f32[16,2,16,2048]{3,2,1,0:T(8,128)S(1)} copy-done((f32[16,2,16,2048]{3,2,1,0:T(8,128)S(1)}, f32[16,2,16,2048]{3,2,1,0:T(8,128)}, u32[]{:S(2)}) %copy-start) | copy-done | bytes 4194328
  2.9 0.0 copy-start.6
  2.9 0.9 copy-done.6
  3.8 0.0 copy-start.1
  3.8 0.0 copy-start.7
  3.8 1.1 %outer_rows.3 = (f32[104,2048]{1,0:T(8,128)S(1)}, f32[104,2048]{1,0:T(8,128)S(1)}) custom-call(s32[1]{0:T(128)} %bitcast.first_row_ref.refs_0_, f32[16,2,16,2048]{3,2,1,0:T(8,128)S(1)} %copy-done, f32[16,2048]{1,0:T(8,128)S(1)} %copy-done.6), custom_call_target="tpu_custom_call" | custom-call | tf_op jit(solution)/shard_map/outer_rows/pallas_call | solution.py:82
  4.9 2.1 %collective-permute-start.2 = (f32[104,2048]{1,0:T(8,128)S(1)}, f32[104,2048]{1,0:T(8,128)S(1)}, u32[]{:S(2)}, u32[]{:S(2)}) collective-permute-start(f32[104,2048]{1,0:T(8,128)S(1)} %get-tuple-element.39), channel_id=1, source_target_pairs={{0,4},{4,0},{8,12},{12,8},{16,20},{20,16},{24,28},{28,24},{32,36},... | collective-permute-start | bytes 2555912 | tf_op jit(solution)/shard_map/ppermute | solution.py:866
  7.0 5.6 %collective-permute-start.3 = (f32[104,2048]{1,0:T(8,128)S(1)}, f32[104,2048]{1,0:T(8,128)S(1)}, u32[]{:S(2)}, u32[]{:S(2)}) collective-permute-start(f32[104,2048]{1,0:T(8,128)S(1)} %get-tuple-element.40), channel_id=1, source_target_pairs={{0,124},{4,8},{8,4},{12,16},{16,12},{20,24},{24,20},{28,32},{32,28... | collective-permute-start | bytes 2555912 | tf_op jit(solution)/shard_map/ppermute | solution.py:867
  12.7 0.0 copy-start.2
  12.7 2.2 %copy-done.2 = f32[16,2,16,2048]{3,2,1,0:T(8,128)S(1)} copy-done((f32[16,2,16,2048]{3,2,1,0:T(8,128)S(1)}, f32[16,2,16,2048]{3,2,1,0:T(8,128)}, u32[]{:S(2)}) %copy-start.2) | copy-done | bytes 4194328
  14.8 0.0 copy-start.3
  14.8 1.1 %outer_rows.2 = (f32[96,2048]{1,0:T(8,128)S(1)}, f32[96,2048]{1,0:T(8,128)S(1)}) custom-call(s32[1]{0:T(128)} %bitcast.first_row_ref.refs_0_, f32[16,2,16,2048]{3,2,1,0:T(8,128)S(1)} %copy-done.2), custom_call_target="tpu_custom_call" | custom-call | tf_op jit(solution)/shard_map/outer_rows/pallas_call | solution.py:82
  15.9 0.1 collective-permute-start
  16.0 0.9 collective-permute-start.1
  16.9 0.0 copy-done.12
  17.0 0.0 copy-done.10
  17.0 0.0 copy-done.9
  17.0 0.0 copy-done.8
  17.0 0.0 copy-done.1
  17.0 0.0 copy-done.7
  17.0 0.0 copy-start.5
  17.0 0.9 %copy-done.5 = f32[16,2,2048]{2,1,0:T(2,128)S(1)} copy-done((f32[16,2,2048]{2,1,0:T(2,128)S(1)}, f32[16,2,2048]{2,1,0:T(2,128)}, u32[]{:S(2)}) %copy-start.5) | copy-done | bytes 262168
  18.0 11.1 %forward_inner.1 = (f32[22,2,16,2048]{3,2,1,0:T(8,128)S(1)}, f32[20,2,16,2048]{3,2,1,0:T(8,128)S(1)}, f32[18,2,16,2048]{3,2,1,0:T(8,128)S(1)}, f32[8,128]{1,0:T(...) custom-call(s32[1]{0:T(128)} %bitcast.first_row_ref.refs_0_, f32[16]{0:T(128)S(1)} %copy-done.8, ...), custom_call_target="tpu_custom_call" | custom-call | tf_op jit(solution)/shard_map/forward_inner/pallas_call | solution.py:587
  29.1 0.0 copy-done.3
  29.1 0.0 copy-start.4
  29.2 10.5 %adjoint_inner.1 = (f32[22,2,16,2048]{3,2,1,0:T(8,128)S(1)}, f32[20,2,16,2048]{3,2,1,0:T(8,128)S(1)}, f32[18,2,16,2048]{3,2,1,0:T(8,128)S(1)}, f32[8,128]{1,0:T(8,128)S(1)}) custom-call(s32[1]{0:T(128)} %bitcast.first_row_ref.refs_0_, f32[16]{0:T(128)S(1)} %copy-done.8, f32[16]{0:T(128)S(1)} %get-tuple-element.60.refs_2_, f32[16]{0:T(128)S(1)} %get-tuple-element.59.refs_3_, ...), custom_call_target="tpu_custom_call" | custom-call | tf_op jit(solution)/shard_map/adjoint_inner/pallas_call | solution.py:587
  39.7 0.0 collective-permute-done.2.refs_6_
  39.7 0.0 collective-permute-done.3.refs_7_
  39.7 0.0 copy-done.4
  39.7 6.3 %forward_outer.1 = (f32[22,2,16,2048]{3,2,1,0:T(8,128)S(1)}, f32[20,2,16,2048]{3,2,1,0:T(8,128)S(1)}, f32[18,2,16,2048]{3,2,1,0:T(8,128)S(1)}, f32[20,16,2048]{2...) custom-call(s32[1]{0:T(128)} %bitcast.first_row_ref.refs_0_, ...), custom_call_target="tpu_custom_call", output_to_operand_aliasing={{0}: (9, {}), {1}: (10, {}), {2}: (11, {}), {3}: (12, {}), ... | custom-call | tf_op jit(solution)/shard_map/forward_outer/pallas_call | solution.py:621
  46.0 0.0 collective-permute-done.refs_6_
  46.1 1.6 %collective-permute-done.1.refs_7_ = f32[96,2048]{1,0:T(8,128)S(1)} collective-permute-done((f32[96,2048]{1,0:T(8,128)S(1)}, f32[96,2048]{1,0:T(8,128)S(1)}, u32[]{:S(2)}, u32[]{:S(2)}) %collective-permute-start.1) | collective-permute-done | bytes 786464 | tf_op jit(solution)/shard_map/ppermute | solution.py:872
  47.7 8.4 %adjoint_outer.1 = (f32[22,2,16,2048]{3,2,1,0:T(8,128)S(1)}, f32[20,2,16,2048]{3,2,1,0:T(8,128)S(1)}, f32[18,2,16,2048]{3,2,1,0:T(8,128)S(1)}, f32[32,8,128]{2,1,0:T(8,128)S(1)}, f32[4,2,16,2048]{3,2,1,0:T(8,128)S(1)}) custom-call(s32[1]{0:T(128)} %bitcast.first_row_ref.refs_0_, ...), custom_call_target="tpu_custom_call", output_to_operand_aliasing={{0}: (9, {}), {1}: (10, {}), {2}: (11, {})} | custom-call | tf_op jit(solution)/shard_map/adjoint_outer/pallas_call | solution.py:621
  56.1 13.0 %all_to_all.5.sums_ref = f32[32,8,128]{2,1,0:T(8,128)S(1)} all-to-all(f32[32,8,128]{2,1,0:T(8,128)S(1)} %get-tuple-element.48), channel_id=1, replica_groups=mesh['gx'=32,'wa'=4] {'gx'}, dimensions={0} | all-to-all | bytes 262144 | tf_op jit(solution)/shard_map/all_to_all | solution.py:906
  69.1 0.0 copy-start.11
  69.1 9.8 %finish.1 = (f32[16,2,16,2048]{3,2,1,0:T(8,128)}, f32[16,2,16,2048]{3,2,1,0:T(8,128)}, f32[16,2048]{1,0:T(8,128)S(1)}, f32[20,2,16,2048]{3,2,1,0:T(8,128)S(1)}, f32[18,2,16,2048]{3,2,1,0:T(8,128)S(1)}) custom-call(s32[1]{0:T(128)} %bitcast.first_row_ref.refs_0_, f32[16]{0:T(128)S(1)} %copy-done.8, ...), custom_call_target="tpu_custom_call", output_to_operand_aliasing={{3}: (8, {}), {4}: (9, {})} | custom-call | tf_op jit(solution)/shard_map/finish/pallas_call | solution.py:785
  78.9 14.0 %all-gather = f32[64,2048]{1,0:T(8,128)S(1)} all-gather(f32[16,2048]{1,0:T(8,128)S(1)} %get-tuple-element.58), channel_id=2, replica_groups=mesh['gx'=32,'wa'=4] {'wa'}, dimensions={0}, use_global_device_ids=true | all-gather | bytes 655360 | tf_op jit(solution)/shard_map/all_gather | solution.py:912
  93.0 0.0 copy-done.11
  93.0 0.7 convert_multiply_fusion
  (2 shorter events, 0.1 us)
Async XLA Ops:
  0.6 16.3 %copy-start.12 = (f32[16]{0:T(128)S(1)}, f32[16]{0:T(128)}, u32[]{:S(2)}) copy-start(f32[16]{0:T(128)} %param.17) | copy-start | bytes 196
  0.6 16.3 %copy-start.10 = (s32[16]{0:T(128)S(1)}, s32[16]{0:T(128)}, u32[]{:S(2)}) copy-start(s32[16]{0:T(128)} %refs_4_.7) | copy-start | bytes 196
  0.7 16.3 %copy-start.9 = (s32[16]{0:T(128)S(1)}, s32[16]{0:T(128)}, u32[]{:S(2)}) copy-start(s32[16]{0:T(128)} %mark_row_ref.1) | copy-start | bytes 196
  0.7 16.3 %copy-start.8 = (f32[16]{0:T(128)S(1)}, f32[16]{0:T(128)}, u32[]{:S(2)}) copy-start(f32[16]{0:T(128)} %squared_k_ref.1) | copy-start | bytes 196
  0.7 2.2 %copy-start = (f32[16,2,16,2048]{3,2,1,0:T(8,128)S(1)}, f32[16,2,16,2048]{3,2,1,0:T(8,128)}, u32[]{:S(2)}) copy-start(f32[16,2,16,2048]{3,2,1,0:T(8,128)} %field_hbm.3) | copy-start | bytes 12582916
  2.9 0.9 copy-start.6
  3.8 13.2 %copy-start.1 = (f32[16,2,16,2048]{3,2,1,0:T(8,128)S(1)}, f32[16,2,16,2048]{3,2,1,0:T(8,128)}, u32[]{:S(2)}) copy-start(f32[16,2,16,2048]{3,2,1,0:T(8,128)} %field_hbm.3) | copy-start | bytes 12582916
  3.8 13.2 %copy-start.7 = (f32[16,2048]{1,0:T(8,128)S(1)}, f32[16,2048]{1,0:T(8,128)}, u32[]{:S(2)}) copy-start(f32[16,2048]{1,0:T(8,128)} %refs_0_.1) | copy-start | bytes 393220
  4.9 34.7 %collective-permute-start.2 = (f32[104,2048]{1,0:T(8,128)S(1)}, f32[104,2048]{1,0:T(8,128)S(1)}, u32[]{:S(2)}, u32[]{:S(2)}) collective-permute-start(f32[104,2048]{1,0:T(8,128)S(1)} %get-tuple-element.39), channel_id=1, source_target_pairs={{0,4},{4,0},{8,12},{12,8},{16,20},{20,16},{24,28},{28,24},{32,36},... | collective-permute-start | bytes 2555912 | tf_op jit(solution)/shard_map/ppermute | solution.py:866
  7.0 32.6 %collective-permute-start.3 = (f32[104,2048]{1,0:T(8,128)S(1)}, f32[104,2048]{1,0:T(8,128)S(1)}, u32[]{:S(2)}, u32[]{:S(2)}) collective-permute-start(f32[104,2048]{1,0:T(8,128)S(1)} %get-tuple-element.40), channel_id=1, source_target_pairs={{0,124},{4,8},{8,4},{12,16},{16,12},{20,24},{24,20},{28,32},{32,28... | collective-permute-start | bytes 2555912 | tf_op jit(solution)/shard_map/ppermute | solution.py:867
  12.7 2.2 %copy-start.2 = (f32[16,2,16,2048]{3,2,1,0:T(8,128)S(1)}, f32[16,2,16,2048]{3,2,1,0:T(8,128)}, u32[]{:S(2)}) copy-start(f32[16,2,16,2048]{3,2,1,0:T(8,128)} %refs_6_.3) | copy-start | bytes 12582916
  14.8 14.3 %copy-start.3 = (f32[16,2,16,2048]{3,2,1,0:T(8,128)S(1)}, f32[16,2,16,2048]{3,2,1,0:T(8,128)}, u32[]{:S(2)}) copy-start(f32[16,2,16,2048]{3,2,1,0:T(8,128)} %refs_6_.3) | copy-start | bytes 12582916
  15.9 30.1 %collective-permute-start = (f32[96,2048]{1,0:T(8,128)S(1)}, f32[96,2048]{1,0:T(8,128)S(1)}, u32[]{:S(2)}, u32[]{:S(2)}) collective-permute-start(f32[96,2048]{1,0:T(8,128)S(1)} %get-tuple-element.31), channel_id=1, source_target_pairs={{0,4},{4,0},{8,12},{12,8},{16,20},{20,16},{24,28},{28,24},{32,36},... | collective-permute-start | bytes 2359304 | tf_op jit(solution)/shard_map/ppermute | solution.py:871
  16.0 31.6 %collective-permute-start.1 = (f32[96,2048]{1,0:T(8,128)S(1)}, f32[96,2048]{1,0:T(8,128)S(1)}, u32[]{:S(2)}, u32[]{:S(2)}) collective-permute-start(f32[96,2048]{1,0:T(8,128)S(1)} %get-tuple-element.32), channel_id=1, source_target_pairs={{0,124},{4,8},{8,4},{12,16},{16,12},{20,24},{24,20},{28,32},{32,28... | collective-permute-start | bytes 2359304 | tf_op jit(solution)/shard_map/ppermute | solution.py:872
  17.0 1.0 %copy-start.5 = (f32[16,2,2048]{2,1,0:T(2,128)S(1)}, f32[16,2,2048]{2,1,0:T(2,128)}, u32[]{:S(2)}) copy-start(f32[16,2,2048]{2,1,0:T(2,128)} %refs_14_.2) | copy-start | bytes 786436
  29.1 10.5 %copy-start.4 = (f32[16,2,2048]{2,1,0:T(2,128)S(1)}, f32[16,2,2048]{2,1,0:T(2,128)}, u32[]{:S(2)}) copy-start(f32[16,2,2048]{2,1,0:T(2,128)} %refs_14_.3) | copy-start | bytes 786436
  69.1 23.9 %copy-start.11 = (s32[16,2048]{1,0:T(8,128)S(1)}, s32[16,2048]{1,0:T(8,128)}, u32[]{:S(2)}) copy-start(s32[16,2048]{1,0:T(8,128)} %param.13) | copy-start | bytes 393220
where the time goes:
time: 92.6 us; the launch traced here: 93.7 us
  Pallas kernels  48.4 us (52%)
  blocking collectives  27.1 us (29%)
  starting transfers between devices  8.72 us (9%)
  local copies, waits for them, and re-layouts  6.31 us (7%)
  waiting for transfers between devices  1.61 us (2%)
    pallas_call x2, Pallas kernels, inner_rows(): pl.pallas_call(functools.partial(inner_kernel, forward=forward, total_row...  21.6 us
    pallas_call x2, Pallas kernels, outer_rows_solve(): pl.pallas_call(functools.partial(outer_kernel, forward=forward, total_row...  14.8 us
    all_gather x1, blocking collectives, local(): summed_terms = lax.all_gather(partial, 'wa').sum(axis=0)  14 us
    all_to_all x1, blocking collectives, local(): lax.all_to_all(sums, 'gx', 0, 0, tiled=True)  13 us
    pallas_call x1, Pallas kernels, finish(): pl.pallas_call(functools.partial(finish_kernel, total_rows=total_rows), i...  9.77 us
    unnamed x26, local copies, waits for them, and re-layouts  6.27 us
    ppermute x1, starting transfers between devices, local(): lax.ppermute(fwd_second, 'gx', pairing_two)  5.62 us
    pallas_call x2, Pallas kernels, outer_rows(): pl.pallas_call(functools.partial(pack_kernel, with_eps=eps is not None),...  2.21 us
  transfers between devices with their start and end apart: 4, of which 1 were waited for; matrix products, arithmetic and copies ran while one was open for 0% of the time, Pallas kernels for 31%

commit v1 on v0

--- a/solution.py
+++ b/solution.py
@@ -18,9 +18,9 @@
 FWD_SUMS = BASE_SUMS + MARK_SUMS
 GROUP_LANES = 64
 TABLE_COLUMNS = 7
-INNER_LIMIT = 6 * 2**20
+INNER_LIMIT = 2 * 2**20
 OUTER_LIMIT = 4 * 2**20
-FINISH_LIMIT = 4 * 2**20
+FINISH_LIMIT = 10 * 2**20
 VMEM = pl.BlockSpec(memory_space=pltpu.VMEM)
 SMEM = pl.BlockSpec(memory_space=pltpu.SMEM)
 HBM = pl.BlockSpec(memory_space=pltpu.HBM)
@@ -34,45 +34,35 @@
     return lax.rem(first_row_ref[0], 2 * rows) != 0
 
 
-def pack_kernel(first_row_ref, field_hbm, *refs, with_eps):
+def pack_kernel(first_row_ref, field_ref, *refs, with_eps):
     if with_eps:
-        eps_ref, first_ref, second_ref, stage_ref, sems = refs
+        eps_ref, first_ref, second_ref = refs
     else:
-        first_ref, second_ref, stage_ref, sems = refs
-    waves, parts, rows, width = field_hbm.shape
+        first_ref, second_ref = refs
+    waves, parts, rows, width = field_ref.shape
     odd = is_odd(first_row_ref, rows)
-    chunks = sems.shape[0]
-    span = width // chunks
-    loads = []
-    for n in range(chunks):
-        lanes = pl.ds(n * span, span)
-        loads.append(
-            pltpu.make_async_copy(
-                field_hbm.at[:, :, :, lanes], stage_ref.at[:, :, :, lanes], sems.at[n]
-            )
-        )
-        loads[-1].start()
+    pieces = [
+        (slice(wave0, wave0 + SUBLANES), part)
+        for wave0 in range(0, waves, SUBLANES)
+        for part in range(parts)
+    ]
     if with_eps:
         at = HALO * parts * waves
         low = jnp.tile(eps_ref[:EPS_ROWS, :], (SUBLANES // EPS_ROWS, 1))
         high = jnp.tile(eps_ref[rows - EPS_ROWS :, :], (SUBLANES // EPS_ROWS, 1))
         first_ref[at : at + SUBLANES, :] = jnp.where(odd, low, high)
         second_ref[at : at + SUBLANES, :] = jnp.where(odd, high, low)
-    for n in range(chunks):
-        loads[n].wait()
-        for part in range(parts):
-            for wave0 in range(0, waves, SUBLANES):
-                for lane0 in range(n * span, (n + 1) * span, LANES):
-                    lanes = slice(lane0, lane0 + LANES)
-                    group = slice(wave0, wave0 + SUBLANES)
-                    head = jnp.swapaxes(stage_ref[group, part, :SUBLANES, lanes], 0, 1)
-                    tail = jnp.swapaxes(stage_ref[group, part, rows - SUBLANES :, lanes], 0, 1)
-                    for k in range(HALO):
-                        at = (k * parts + part) * waves + wave0
-                        low = head[k]
-                        high = tail[SUBLANES - HALO + k]
-                        first_ref[at : at + SUBLANES, lanes] = jnp.where(odd, low, high)
-                        second_ref[at : at + SUBLANES, lanes] = jnp.where(odd, high, low)
+    for group, part in pieces:
+        for lane0 in range(0, width, LANES):
+            lanes = slice(lane0, lane0 + LANES)
+            head = jnp.swapaxes(field_ref[group, part, :SUBLANES, lanes], 0, 1)
+            tail = jnp.swapaxes(field_ref[group, part, rows - SUBLANES :, lanes], 0, 1)
+            for k in range(HALO):
+                at = (k * parts + part) * waves + group.start
+                low = head[k]
+                high = tail[SUBLANES - HALO + k]
+                first_ref[at : at + SUBLANES, lanes] = jnp.where(odd, low, high)
+                second_ref[at : at + SUBLANES, lanes] = jnp.where(odd, high, low)
 
 
 def outer_rows(first_row, field, eps=None):
@@ -81,14 +71,12 @@
     shape = jax.ShapeDtypeStruct((height, width), jnp.float32)
     return pl.pallas_call(
         functools.partial(pack_kernel, with_eps=eps is not None),
-        in_specs=[SMEM, HBM] + ([] if eps is None else [VMEM]),
+        in_specs=[SMEM, VMEM] + ([] if eps is None else [VMEM]),
         out_specs=[VMEM, VMEM],
         out_shape=[shape, shape],
-        scratch_shapes=[
-            pltpu.VMEM(field.shape, jnp.float32),
-            pltpu.SemaphoreType.DMA((8,)),
-        ],
-        compiler_params=pltpu.CompilerParams(vmem_limit_bytes=INNER_LIMIT),
+        compiler_params=pltpu.CompilerParams(
+            vmem_limit_bytes=INNER_LIMIT
+        ),
         name="outer_rows",
     )(first_row, field, *(() if eps is None else (eps,)))
 
@@ -116,6 +104,28 @@
         tile, up_before, down_here = following, up_here, down_after
 
 
+class Scalars:
+    def __init__(self, whole_ref, real_ref):
+        self.whole, self.real = whole_ref, real_ref
+        self.waves = real_ref.shape[0] // 3
+        self.first_row = whole_ref[0]
+
+    def source(self, w):
+        return self.whole[1 + w]
+
+    def monitor(self, w):
+        return self.whole[1 + self.waves + w]
+
+    def squared_k(self, w):
+        return self.real[w]
+
+    def cosine(self, w):
+        return self.real[self.waves + w]
+
+    def sine(self, w):
+        return self.real[2 * self.waves + w]
+
+
 class Rows:
     def __init__(self, x_ref, z_ref, u_ref, diag_ref, inv_ref, wave_ref):
         self.x, self.z, self.u = x_ref, z_ref, u_ref
@@ -139,58 +149,66 @@
                 self.diag[i, group, lanes] = diagonal
                 self.inv[i, group, lanes] = 1.0 / diagonal
 
-    def residual(self, i):
-        for group in self.groups():
-            both = [
+    def tiles_of(self, ref, i, count, group):
+        chains = [
+            [
                 lane_neighbours(
-                    lambda j, part=part: self.x[i + 1, part, group, lane_slice(j)], self.tiles
+                    lambda j, at=i + k, part=part: ref[at, part, group, lane_slice(j)], self.tiles
                 )
                 for part in range(self.parts)
             ]
-            for steps in zip(*both):
-                for part, (j, centre, sides) in enumerate(steps):
-                    lanes = lane_slice(j)
-                    around = self.x[i, part, group, lanes] + self.x[i + 2, part, group, lanes]
-                    self.z[i, part, group, lanes] = (
-                        around + sides - self.diag[i, group, lanes] * centre
-                    ) * self.inv[i, group, lanes]
-
-    def image(self, i):
+            for k in range(count)
+        ]
+        for j in range(self.tiles):
+            lanes = lane_slice(j)
+            now = [[next(chain)[1:] for chain in row] for row in chains]
+            out = []
+            for k in range(count):
+                row = []
+                for part in range(self.parts):
+                    low = now[k - 1][part][0] if k else ref[i - 1, part, group, lanes]
+                    high = now[k + 1][part][0] if k + 1 < count else ref[i + count, part, group, lanes]
+                    centre, sides = now[k][part]
+                    row.append((centre, low + high, sides))
+                out.append(row)
+            yield j, out
+
+    def residual(self, i, count):
         for group in self.groups():
-            both = [
-                lane_neighbours(
-                    lambda j, part=part: self.z[i + 1, part, group, lane_slice(j)], self.tiles
-                )
-                for part in range(self.parts)
-            ]
-            for steps in zip(*both):
-                for part, (j, centre, sides) in enumerate(steps):
-                    lanes = lane_slice(j)
-                    around = self.z[i, part, group, lanes] + self.z[i + 2, part, group, lanes]
-                    image = self.diag[i + 1, group, lanes] * centre - (around + sides)
-                    self.u[i, part, group, lanes] = image * self.inv[i + 1, group, lanes]
-
-    def vectors(self, i, group):
-        both = [
-            lane_neighbours(
-                lambda j, part=part: self.u[i + 1, part, group, lane_slice(j)], self.tiles
-            )
-            for part in range(self.parts)
-        ]
-        for steps in zip(*both):
-            lanes = lane_slice(steps[0][0])
-            diagonal = self.diag[i + 2, group, lanes]
-            r, v, w = [], [], []
-            for part, (_, centre, sides) in enumerate(steps):
-                r.append(diagonal * self.z[i + 2, part, group, lanes])
-                v.append(diagonal * centre)
-                around = self.u[i, part, group, lanes] + self.u[i + 2, part, group, lanes]
-                w.append(v[-1] - (around + sides))
-            yield steps[0][0], r, v, w
-
-    def twice(self, i, group, sums):
+            for j, block in self.tiles_of(self.x, i + 1, count, group):
+                lanes = lane_slice(j)
+                for k in range(count):
+                    diagonal = self.diag[i + k, group, lanes]
+                    inverse = self.inv[i + k, group, lanes]
+                    for part, (centre, around, sides) in enumerate(block[k]):
+                        self.z[i + k, part, group, lanes] = (
+                            around + sides - diagonal * centre
+                        ) * inverse
+
+    def image(self, i, count):
+        for group in self.groups():
+            for j, block in self.tiles_of(self.z, i + 1, count, group):
+                lanes = lane_slice(j)
+                for k in range(count):
+                    inverse = self.inv[i + 1 + k, group, lanes]
+                    for part, (centre, around, sides) in enumerate(block[k]):
+                        self.u[i + k, part, group, lanes] = centre - (around + sides) * inverse
+
+    def vectors(self, i, group, count=1):
+        for j, block in self.tiles_of(self.u, i + 1, count, group):
+            lanes = lane_slice(j)
+            for k in range(count):
+                diagonal = self.diag[i + 2 + k, group, lanes]
+                r, v, w = [], [], []
+                for part, (centre, around, sides) in enumerate(block[k]):
+                    r.append(diagonal * self.z[i + 2 + k, part, group, lanes])
+                    v.append(diagonal * centre)
+                    w.append(v[-1] - (around + sides))
+                yield j, r, v, w
+
+    def twice(self, i, group, sums, count):
         rr, rv_re, rv_im, vv, wr_re, wr_im, wv_re, wv_im, ww = sums
-        for _, r, v, w in self.vectors(i, group):
+        for _, r, v, w in self.vectors(i, group, count):
             rr += r[0] * r[0] + r[1] * r[1]
             rv_re += r[0] * v[0] + r[1] * v[1]
             rv_im += r[0] * v[1] - r[1] * v[0]
@@ -202,18 +220,18 @@
             ww += w[0] * w[0] + w[1] * w[1]
         return rr, rv_re, rv_im, vv, wr_re, wr_im, wv_re, wv_im, ww
 
-    def any_at(self, table_ref, row):
-        hit = table_ref[0] == row
+    def any_at(self, row_of, row):
+        hit = row_of(0) == row
         for w in range(1, self.waves):
-            hit = jnp.logical_or(hit, table_ref[w] == row)
+            hit = jnp.logical_or(hit, row_of(w) == row)
         return hit
 
-    def source(self, i, first_row, total_rows, side_row_ref, side_ref):
-        row = first_row + i - 2
+    def source(self, i, scalars, total_rows, side_ref):
+        row = scalars.first_row + i - 2
         row = jnp.where(row < 0, row + total_rows, row)
         row = jnp.where(row >= total_rows, row - total_rows, row)
 
-        @pl.when(self.any_at(side_row_ref, row))
+        @pl.when(self.any_at(scalars.source, row))
         def _():
             for group in self.groups():
                 cosine, sine = self.frame(i - 2, group)
@@ -239,29 +257,28 @@
         )
 
 
-def wave_column(ref, wave0):
+def wave_column(value_of, wave0):
     sublane = lax.broadcasted_iota(jnp.int32, (SUBLANES, LANES), 0)
     out = jnp.zeros((SUBLANES, LANES), jnp.float32)
     for k in range(SUBLANES):
-        out = jnp.where(sublane == k, ref[wave0 + k].astype(jnp.float32), out)
+        out = jnp.where(sublane == k, value_of(wave0 + k).astype(jnp.float32), out)
     return out
 
 
-def fill_table(table_ref, wave_refs, first_row, rows, total_rows, sign):
-    squared_k_ref, cosine_ref, sine_ref, source_ref, monitor_ref = wave_refs
-    at_first = first_row == 0
-    at_last = first_row == total_rows - rows
+def fill_table(table_ref, scalars, rows, total_rows, sign):
+    at_first = scalars.first_row == 0
+    at_last = scalars.first_row == total_rows - rows
     for wave0 in range(0, table_ref.shape[1], SUBLANES):
         group = slice(wave0, wave0 + SUBLANES)
-        cosine = wave_column(cosine_ref, wave0)
-        sine = sign * wave_column(sine_ref, wave0)
-        table_ref[0, group, :] = wave_column(squared_k_ref, wave0)
+        cosine = wave_column(scalars.cosine, wave0)
+        sine = sign * wave_column(scalars.sine, wave0)
+        table_ref[0, group, :] = wave_column(scalars.squared_k, wave0)
         table_ref[1, group, :] = jnp.where(at_first, cosine, 1.0)
         table_ref[2, group, :] = jnp.where(at_first, -sine, 0.0)
         table_ref[3, group, :] = jnp.where(at_last, cosine, 1.0)
         table_ref[4, group, :] = jnp.where(at_last, sine, 0.0)
-        table_ref[5, group, :] = wave_column(source_ref, wave0)
-        table_ref[6, group, :] = wave_column(monitor_ref, wave0)
+        table_ref[5, group, :] = wave_column(scalars.source, wave0)
+        table_ref[6, group, :] = wave_column(scalars.monitor, wave0)
 
 
 def lanes_of(out, totals, wave0, offset):
@@ -273,66 +290,55 @@
 
 
 def inner_kernel(*refs, forward, total_rows):
-    first_row_ref, *wave_refs = refs[:6]
-    field_hbm, refs = refs[6], refs[7:]
-    side_row_ref = wave_refs[3]
+    scalars = Scalars(*refs[:2])
+    field_ref, refs = refs[2], refs[3:]
     if forward:
         (eps_ref, side_ref) = refs[:2]
-        (x_ref, z_ref, u_ref, sums_ref, diag_ref, inv_ref, stage_ref, table_ref, sems) = refs[2:]
+        (x_ref, z_ref, u_ref, sums_ref, diag_ref, inv_ref, table_ref) = refs[2:]
     else:
         (diag_ref, inv_ref) = refs[:2]
-        (x_ref, z_ref, u_ref, sums_ref, stage_ref, table_ref, sems) = refs[2:]
+        (x_ref, z_ref, u_ref, sums_ref, table_ref) = refs[2:]
     step = Rows(x_ref, z_ref, u_ref, diag_ref, inv_ref, table_ref)
     rows, waves = step.rows, step.waves
-    chunks = sems.shape[0]
-    span = step.tiles * LANES // chunks
-    loads = []
-    for n in range(chunks):
-        lanes = pl.ds(n * span, span)
-        loads.append(
-            pltpu.make_async_copy(
-                field_hbm.at[:, :, :, lanes], stage_ref.at[:, :, :, lanes], sems.at[n]
-            )
-        )
-        loads[-1].start()
-    fill_table(
-        table_ref, wave_refs, first_row_ref[0], rows, total_rows, 1.0 if forward else -1.0
-    )
+    fill_table(table_ref, scalars, rows, total_rows, 1.0 if forward else -1.0)
     if forward:
         for row in range(rows):
             step.set_diagonal(row + 2, lambda lanes, row=row: eps_ref[row : row + 1, lanes])
-    for n in range(chunks):
-        loads[n].wait()
+    def turn(j, _):
+        lanes = pl.ds(pl.multiple_of(j * LANES, LANES), LANES)
         for part in range(step.parts):
             for group in step.groups():
                 for row0 in range(0, rows, SUBLANES):
-                    for lane0 in range(n * span, (n + 1) * span, LANES):
-                        lanes = slice(lane0, lane0 + LANES)
-                        x_ref[HALO + row0 : HALO + row0 + SUBLANES, part, group, lanes] = (
-                            jnp.swapaxes(
-                                stage_ref[group, part, row0 : row0 + SUBLANES, lanes], 0, 1
-                            )
+                    x_ref[HALO + row0 : HALO + row0 + SUBLANES, part, group, lanes] = (
+                        jnp.swapaxes(
+                            field_ref[group, part, row0 : row0 + SUBLANES, lanes], 0, 1
                         )
-
-    def residual(i, _):
-        step.residual(i)
+                    )
+        return 0
+
+    lax.fori_loop(0, step.tiles, turn, 0)
+
+    def residual(t, _):
+        i = 3 + 2 * t
+        step.residual(i, 2)
         if forward:
-            step.source(i, first_row_ref[0], total_rows, side_row_ref, side_ref)
+            step.source(i, scalars, total_rows, side_ref)
+            step.source(i + 1, scalars, total_rows, side_ref)
         return 0
 
-    def image(i, _):
-        step.image(i)
+    def image(t, _):
+        step.image(3 + 3 * t, 3)
         return 0
 
-    lax.fori_loop(3, rows + 1, residual, 0)
-    lax.fori_loop(3, rows - 1, image, 0)
+    lax.fori_loop(0, (rows - 2) // 2, residual, 0)
+    lax.fori_loop(0, (rows - 4) // 3, image, 0)
     zero = jnp.zeros((SUBLANES, LANES), jnp.float32)
     out = zero
     for group in step.groups():
         sums = lax.fori_loop(
-            3,
-            rows - 3,
-            lambda i, sums, group=group: step.twice(i, group, sums),
+            0,
+            (rows - 6) // 2,
+            lambda t, sums, group=group: step.twice(3 + 2 * t, group, sums, 2),
             (zero,) * BASE_SUMS,
         )
         out = lanes_of(out, sums, group.start, 0 if forward else FWD_SUMS)
@@ -340,20 +346,19 @@
 
 
 def outer_kernel(*refs, forward, total_rows):
-    first_row_ref, *wave_refs = refs[:6]
-    row_ref, mark_row_ref = wave_refs[3:]
-    first_ref, second_ref = refs[6:8]
+    scalars = Scalars(*refs[:2])
+    first_ref, second_ref, refs = refs[2], refs[3], refs[4:]
     if forward:
-        (part_ref, _, _, _, _, _, side_ref, mark_ref) = refs[8:16]
-        (x_ref, z_ref, u_ref, diag_ref, inv_ref, sums_ref, table_ref, mark_sums) = refs[16:]
+        (part_ref, _, _, _, _, _, side_ref, mark_ref) = refs[:8]
+        (x_ref, z_ref, u_ref, diag_ref, inv_ref, sums_ref, table_ref, mark_sums) = refs[8:]
     else:
-        (part_ref, _, _, _, diag_ref, inv_ref, mark_ref, fwd_sums_ref) = refs[8:16]
-        (x_ref, z_ref, u_ref, sums_ref, line_ref, table_ref, line_sums, g_ref) = refs[16:]
+        (part_ref, _, _, _, diag_ref, inv_ref, mark_ref, fwd_sums_ref) = refs[:8]
+        (x_ref, z_ref, u_ref, sums_ref, line_ref, table_ref, line_sums, g_ref) = refs[8:]
     step = Rows(x_ref, z_ref, u_ref, diag_ref, inv_ref, table_ref)
     rows, parts, waves, tiles = step.rows, step.parts, step.waves, step.tiles
-    odd = is_odd(first_row_ref, rows)
-    first_row = first_row_ref[0]
-    fill_table(table_ref, wave_refs, first_row, rows, total_rows, 1.0 if forward else -1.0)
+    first_row = scalars.first_row
+    odd = lax.rem(first_row, 2 * rows) != 0
+    fill_table(table_ref, scalars, rows, total_rows, 1.0 if forward else -1.0)
     for group in step.groups():
         for base, offset, swap in ((0, 1, False), (HALO + rows, 3, True)):
             cosine = step.column(offset, group)
@@ -385,30 +390,28 @@
             step.set_diagonal(k, above_eps)
             step.set_diagonal(rows + 2 + k, below_eps)
 
-    def outer(t, count):
-        return jnp.where(t < 3, t, t + count - 6)
-
     def residual(t, _):
-        i = outer(t, rows + 4)
-        step.residual(i)
+        i = t * (rows + 1)
+        step.residual(i, 3)
         if forward:
-            step.source(i, first_row, total_rows, row_ref, side_ref)
+            for k in range(3):
+                step.source(i + k, scalars, total_rows, side_ref)
         return 0
 
     def image(t, _):
-        step.image(outer(t, rows + 2))
+        step.image(t * (rows - 1), 3)
         return 0
 
-    lax.fori_loop(0, 6, residual, 0)
-    lax.fori_loop(0, 6, image, 0)
+    lax.fori_loop(0, 2, residual, 0)
+    lax.fori_loop(0, 2, image, 0)
     zero = jnp.zeros((SUBLANES, LANES), jnp.float32)
     base_sums = []
     for group in step.groups():
         base_sums.append(
             lax.fori_loop(
                 0,
-                6,
-                lambda t, sums, group=group: step.twice(outer(t, rows), group, sums),
+                2,
+                lambda t, sums, group=group: step.twice(t * (rows - 3), group, sums, 3),
                 (zero,) * BASE_SUMS,
             )
         )
@@ -418,7 +421,7 @@
         def mark_at(i, _):
             row = first_row + i
 
-            @pl.when(step.any_at(mark_row_ref, row))
+            @pl.when(step.any_at(scalars.monitor, row))
             def _():
                 for group in step.groups():
                     chosen = step.column(6, group) == row.astype(jnp.float32)
@@ -437,7 +440,7 @@
         lax.fori_loop(0, rows, mark_at, 0)
         extra, count = mark_sums, MARK_SUMS
     else:
-        line_terms(step, first_row, total_rows, mark_row_ref, mark_ref, line_ref, line_sums, g_ref)
+        line_terms(step, scalars, total_rows, mark_ref, line_ref, line_sums, g_ref)
         extra, count = line_sums, LINE_SUMS
     out = part_ref[...]
     new = jnp.zeros((SUBLANES, LANES), jnp.float32)
@@ -463,14 +466,14 @@
     return a[0] * b[0] + a[1] * b[1], a[0] * b[1] - a[1] * b[0]
 
 
-def line_terms(step, first_row, total_rows, mark_row_ref, mark_ref, line_ref, line_sums, g_ref):
+def line_terms(step, scalars, total_rows, mark_ref, line_ref, line_sums, g_ref):
     rows, tiles = step.rows, step.tiles
     line_ref[...] = jnp.zeros_like(line_ref)
     line_sums[...] = jnp.zeros_like(line_sums)
     sublane = lax.broadcasted_iota(jnp.int32, (SUBLANES, LANES), 0)
 
     def one_wave(w, _):
-        away = distance_to(mark_row_ref[w], first_row, total_rows)
+        away = distance_to(scalars.monitor(w), scalars.first_row, total_rows)
 
         @pl.when(away <= rows + 1)
         def _():
@@ -586,15 +589,15 @@
         out_shape += [array(rows + 4, waves, width)] * 2
     return pl.pallas_call(
         functools.partial(inner_kernel, forward=forward, total_rows=total_rows),
-        in_specs=[SMEM] * 6 + [HBM, VMEM, VMEM],
+        in_specs=[SMEM] * 2 + [VMEM, VMEM, VMEM],
         out_specs=[VMEM] * len(out_shape),
         out_shape=out_shape,
         scratch_shapes=[
-            pltpu.VMEM((waves, parts, rows, width), jnp.float32),
             pltpu.VMEM((TABLE_COLUMNS, waves, LANES), jnp.float32),
-            pltpu.SemaphoreType.DMA((4,)),
         ],
-        compiler_params=pltpu.CompilerParams(vmem_limit_bytes=INNER_LIMIT),
+        compiler_params=pltpu.CompilerParams(
+            vmem_limit_bytes=INNER_LIMIT
+        ),
         name="forward_inner" if forward else "adjoint_inner",
     )(*args)
 
@@ -606,21 +609,21 @@
     scratch = [pltpu.VMEM((TABLE_COLUMNS, waves, LANES), jnp.float32)]
     if forward:
         out_shape = [array(*a.shape) for a in (x, z, u, diag, inv, sums)]
-        aliases = {9: 0, 10: 1, 11: 2, 12: 3, 13: 4}
+        aliases = {5: 0, 6: 1, 7: 2, 8: 3, 9: 4}
         scratch += [pltpu.VMEM((MARK_SUMS, waves, LANES), jnp.float32)]
     else:
         out_shape = [array(*a.shape) for a in (x, z, u)] + [
             array(copies, SUBLANES, LANES),
             array(4, 2, waves, x.shape[-1]),
         ]
-        aliases = {9: 0, 10: 1, 11: 2}
+        aliases = {5: 0, 6: 1, 7: 2}
         scratch += [
             pltpu.VMEM((LINE_SUMS, waves, LANES), jnp.float32),
             pltpu.VMEM((6, 2, SUBLANES, x.shape[-1]), jnp.float32),
         ]
     return pl.pallas_call(
         functools.partial(outer_kernel, forward=forward, total_rows=total_rows),
-        in_specs=[SMEM] * 6 + [VMEM] * (len(args) - 6),
+        in_specs=[SMEM] * 2 + [VMEM] * (len(args) - 2),
         out_specs=[VMEM] * len(out_shape),
         out_shape=out_shape,
         scratch_shapes=scratch,
@@ -631,9 +634,8 @@
 
 
 def finish_kernel(
-    first_row_ref,
-    squared_k_ref,
-    mark_row_ref,
+    whole_ref,
+    real_ref,
     sums_ref,
     xf_ref,
     zf_ref,
@@ -657,6 +659,7 @@
     waves, parts, rows, width = fwd_hbm.shape
     tiles = width // LANES
     groups = [slice(w, w + SUBLANES) for w in range(0, waves, SUBLANES)]
+    scalars = Scalars(whole_ref, real_ref)
 
     def column(index, group):
         return coef_ref[index, group, :]
@@ -677,12 +680,12 @@
         adj_coefs = step_lengths(
             *with_line(adj_cols[:BASE_SUMS], adj_cols[BASE_SUMS:], over_re, -over_im)
         )
-        twice_k = 2.0 * wave_column(squared_k_ref, group.start)
+        twice_k = 2.0 * wave_column(scalars.squared_k, group.start)
         for n, value in enumerate((*fwd_coefs, *adj_coefs, twice_k, over_re, -over_im)):
             coef_ref[n, group, :] = value
 
     def one_wave(w, _):
-        away = distance_to(mark_row_ref[w], first_row_ref[0], total_rows)
+        away = distance_to(scalars.monitor(w), scalars.first_row, total_rows)
 
         @pl.when(away <= rows)
         def _():
@@ -708,29 +711,15 @@
     lax.fori_loop(0, waves, one_wave, 0)
     sublane = lax.broadcasted_iota(jnp.int32, (SUBLANES, LANES), 0)
 
-    def copies(j, slot):
-        at = pl.ds(j * LANES, LANES)
-        if not isinstance(j, int):
-            at = pl.ds(pl.multiple_of(j * LANES, LANES), LANES)
-        return [
-            pltpu.make_async_copy(fwd_stage.at[slot], fwd_hbm.at[:, :, :, at], sems.at[slot, 0]),
-            pltpu.make_async_copy(adj_stage.at[slot], adj_hbm.at[:, :, :, at], sems.at[slot, 1]),
-        ]
-
-    def tile_step(j, _):
-        slot = lax.rem(j, 2)
-        lanes = pl.ds(pl.multiple_of(j * LANES, LANES), LANES)
-
-        @pl.when(j >= 2)
-        def _():
-            for copy in copies(j - 2, slot):
-                copy.wait()
-
-        for row0 in range(0, rows, SUBLANES):
-            terms = [jnp.zeros((SUBLANES, LANES), jnp.float32)] * SUBLANES
-            for group in groups:
+    copies = []
+    for row0 in range(0, rows, SUBLANES):
+        for group in groups:
+
+            def tile_step(j, row0=row0, group=group):
+                lanes = pl.ds(pl.multiple_of(j * LANES, LANES), LANES)
                 coefs = [column(n, group) for n in range(9)]
                 results = [[], [], [], []]
+                out = jnp.zeros((SUBLANES, LANES), jnp.float32)
                 for k in range(SUBLANES):
                     row = row0 + k
                     values = []
@@ -754,46 +743,51 @@
                             + (b_re * u_im + b_im * u_re)
                         )
                     f_re, f_im, g_re, g_im = values
-                    terms[k] = terms[k] + coefs[8] * (g_re * f_re - g_im * f_im)
+                    term = coefs[8] * (g_re * f_re - g_im * f_im)
+                    out = jnp.where(sublane == k, jnp.sum(term, axis=0, keepdims=True), out)
                     for n in range(4):
                         results[n].append(values[n])
                 for n, (ref, part) in enumerate(
                     ((fwd_stage, 0), (fwd_stage, 1), (adj_stage, 0), (adj_stage, 1))
                 ):
-                    ref[slot, group, part, row0 : row0 + SUBLANES, :] = jnp.swapaxes(
+                    ref[group, part, row0 : row0 + SUBLANES, lanes] = jnp.swapaxes(
                         jnp.stack(results[n]), 0, 1
                     )
-            out = jnp.zeros((SUBLANES, LANES), jnp.float32)
-            for k in range(SUBLANES):
-                out = jnp.where(sublane == k, jnp.sum(terms[k], axis=0, keepdims=True), out)
-            grad_ref[row0 : row0 + SUBLANES, lanes] = out
-        for copy in copies(j, slot):
-            copy.start()
-        return 0
-
-    lax.fori_loop(0, tiles, tile_step, 0)
-    for j in (tiles - 2, tiles - 1):
-        for copy in copies(j, j % 2):
-            copy.wait()
+                if group.start:
+                    out = out + grad_ref[row0 : row0 + SUBLANES, lanes]
+                grad_ref[row0 : row0 + SUBLANES, lanes] = out
+
+            def two_tiles(t, _, tile_step=tile_step):
+                tile_step(2 * t)
+                tile_step(2 * t + 1)
+                return 0
+
+            lax.fori_loop(0, tiles // 2, two_tiles, 0)
+            at = pl.ds(group.start, SUBLANES), slice(None), pl.ds(row0, SUBLANES)
+            for stage, hbm in ((fwd_stage, fwd_hbm), (adj_stage, adj_hbm)):
+                copies.append(pltpu.make_async_copy(stage.at[at], hbm.at[at], sems.at[len(copies)]))
+                copies[-1].start()
+    for copy in copies:
+        copy.wait()
 
 
 def finish(scalars, sums, forward_parts, adjoint_parts, line, total_rows):
     x, z, u = forward_parts
     rows, parts, waves, width = x.shape[0] - 2 * HALO, *x.shape[1:]
     field = array(waves, parts, rows, width)
-    stage = pltpu.VMEM((2, waves, parts, rows, LANES), jnp.float32)
+    stage = pltpu.VMEM((waves, parts, rows, width), jnp.float32)
     return pl.pallas_call(
         functools.partial(finish_kernel, total_rows=total_rows),
-        in_specs=[SMEM] * 3 + [VMEM] * 8,
+        in_specs=[SMEM] * 2 + [VMEM] * 8,
         out_specs=[HBM, HBM, VMEM, VMEM, VMEM],
         out_shape=[field, field, array(rows, width), array(*z.shape), array(*u.shape)],
         scratch_shapes=[
             pltpu.VMEM((11, waves, LANES), jnp.float32),
             stage,
             stage,
-            pltpu.SemaphoreType.DMA((2, 2)),
+            pltpu.SemaphoreType.DMA((8,)),
         ],
-        input_output_aliases={8: 3, 9: 4},
+        input_output_aliases={7: 3, 8: 4},
         compiler_params=pltpu.CompilerParams(vmem_limit_bytes=FINISH_LIMIT),
         name="finish",
     )(*scalars, sums, *forward_parts, *adjoint_parts, line)[:3]
@@ -872,12 +866,8 @@
         lax.ppermute(adj_second, "gx", pairing_two),
     )
     scalars = (
-        first_row,
-        wavenumber,
-        jnp.cos(bloch_phase),
-        jnp.sin(bloch_phase),
-        source_row,
-        monitor_row,
+        jnp.concatenate([first_row, source_row, monitor_row]),
+        jnp.concatenate([wavenumber, jnp.cos(bloch_phase), jnp.sin(bloch_phase)]),
     )
     fx, fz, fu, f_sums, diag, inv = inner_rows(
         True, warm_field, scalars, (permittivity, source_profile), total_rows
@@ -902,7 +892,7 @@
         total_rows,
     )
     forward, adjoint, partial = finish(
-        (first_row, wavenumber, monitor_row),
+        scalars,
         lax.all_to_all(sums, "gx", 0, 0, tiled=True),
         (fx, fz, fu),
         (ax, az, au),

time: 92.6 us -> 90.4 us (0.976); the launches traced: 93.7 us -> 89.2 us
  Pallas kernels: 48.4 us -> 38.7 us
  waiting for transfers between devices: 1.61 us -> 9.27 us
  local copies, waits for them, and re-layouts: 6.31 us -> 4.46 us
    ppermute x1, waiting for transfers between devices: 1.6 us -> 5.54 us  [local(): lax.ppermute(adj_second, 'gx', pairing_two)]
    pallas_call x2, Pallas kernels: 21.6 us -> 17.9 us  [inner_rows(): pl.pallas_call(functools.partial(inner_kernel, forward=forward, total_row...]
    ppermute x1, waiting for transfers between devices: 0.01 us -> 3.73 us  [local(): lax.ppermute(adj_first, 'gx', pairing_one)]
    all_gather x1, blocking collectives: 14 us -> 10.9 us  [local(): summed_terms = lax.all_gather(partial, 'wa').sum(axis=0)]
    pallas_call x2, Pallas kernels: 14.8 us -> 11.7 us  [outer_rows_solve(): pl.pallas_call(functools.partial(outer_kernel, forward=forward, total_row...]
    all_to_all x1, blocking collectives: 13 us -> 15.5 us  [local(): lax.all_to_all(sums, 'gx', 0, 0, tiled=True)]
    unnamed x26, local copies, waits for them, and re-layouts: 6.27 us -> 4.42 us
    pallas_call x1, Pallas kernels: 9.77 us -> 8.39 us  [finish(): pl.pallas_call(functools.partial(finish_kernel, total_rows=total_rows), i...]
  transfers between devices with their start and end apart: 4 -> 4, of which waited for: 1 -> 2; matrix products, arithmetic and copies ran while one was open for 0% -> 0% of each run, Pallas kernels for 31% -> 26%
where the time goes in v1:
time: 90.4 us; the launch traced here: 89.2 us
  Pallas kernels  38.7 us (43%)
  blocking collectives  26.4 us (29%)
  waiting for transfers between devices  9.27 us (10%)
  starting transfers between devices  8.72 us (10%)
  local copies, waits for them, and re-layouts  4.46 us (5%)
    pallas_call x2, Pallas kernels, inner_rows(): pl.pallas_call(functools.partial(inner_kernel, forward=forward, total_row...  17.9 us
    all_to_all x1, blocking collectives, local(): lax.all_to_all(sums, 'gx', 0, 0, tiled=True)  15.5 us
    pallas_call x2, Pallas kernels, outer_rows_solve(): pl.pallas_call(functools.partial(outer_kernel, forward=forward, total_row...  11.7 us
    all_gather x1, blocking collectives, local(): summed_terms = lax.all_gather(partial, 'wa').sum(axis=0)  10.9 us
    pallas_call x1, Pallas kernels, finish(): pl.pallas_call(functools.partial(finish_kernel, total_rows=total_rows), i...  8.39 us
    ppermute x1, starting transfers between devices, local(): lax.ppermute(fwd_second, 'gx', pairing_two)  5.62 us
    ppermute x1, waiting for transfers between devices, local(): lax.ppermute(adj_second, 'gx', pairing_two)  5.54 us
    unnamed x26, local copies, waits for them, and re-layouts  4.42 us
  transfers between devices with their start and end apart: 4, of which 2 were waited for; matrix products, arithmetic and copies ran while one was open for 0% of the time, Pallas kernels for 26%

profile of v1, /device:TPU:1, one launch (start us, length us, event | category | flops | bytes accessed | tf_op | source)
XLA Modules:
  0.0 89.2 jit_solution(9692851697314409654)
XLA Ops:
  0.6 0.0 copy-start.10
  0.6 0.0 copy-start.9
  0.7 0.0 copy-start.12
  0.7 0.0 copy-start.11
  0.7 0.0 copy-start
  0.7 0.0 copy-start.1
  0.7 2.3 %copy-done.1 = f32[16,2,16,2048]{3,2,1,0:T(8,128)S(1)} copy-done((f32[16,2,16,2048]{3,2,1,0:T(8,128)S(1)}, f32[16,2,16,2048]{3,2,1,0:T(8,128)}, u32[]{:S(2)}) %copy-start.1) | copy-done | bytes 4194328
  3.0 0.0 copy-start.6
  3.0 1.1 %copy-done.6 = f32[16,2048]{1,0:T(8,128)S(1)} copy-done((f32[16,2048]{1,0:T(8,128)S(1)}, f32[16,2048]{1,0:T(8,128)}, u32[]{:S(2)}) %copy-start.6) | copy-done | bytes 131096
  4.1 0.0 copy-start.2
  4.1 0.0 copy-start.7
  4.1 0.4 outer_rows.3
  4.6 2.1 %collective-permute-start.2 = (f32[104,2048]{1,0:T(8,128)S(1)}, f32[104,2048]{1,0:T(8,128)S(1)}, u32[]{:S(2)}, u32[]{:S(2)}) collective-permute-start(f32[104,2048]{1,0:T(8,128)S(1)} %get-tuple-element.39), channel_id=1, source_target_pairs={{0,4},{4,0},{8,12},{12,8},{16,20},{20,16},{24,28},{28,24},{32,36},... | collective-permute-start | bytes 2555912 | tf_op jit(solution)/shard_map/ppermute | solution.py:860
  6.7 5.6 %collective-permute-start.3 = (f32[104,2048]{1,0:T(8,128)S(1)}, f32[104,2048]{1,0:T(8,128)S(1)}, u32[]{:S(2)}, u32[]{:S(2)}) collective-permute-start(f32[104,2048]{1,0:T(8,128)S(1)} %get-tuple-element.40), channel_id=1, source_target_pairs={{0,124},{4,8},{8,4},{12,16},{16,12},{20,24},{24,20},{28,32},{32,28... | collective-permute-start | bytes 2555912 | tf_op jit(solution)/shard_map/ppermute | solution.py:861
  12.3 0.0 copy-done
  12.3 0.4 outer_rows.2
  12.7 0.1 collective-permute-start
  12.8 0.9 %collective-permute-start.1 = (f32[96,2048]{1,0:T(8,128)S(1)}, f32[96,2048]{1,0:T(8,128)S(1)}, u32[]{:S(2)}, u32[]{:S(2)}) collective-permute-start(f32[96,2048]{1,0:T(8,128)S(1)} %get-tuple-element.32), channel_id=1, source_target_pairs={{0,124},{4,8},{8,4},{12,16},{16,12},{20,24},{24,20},{28,32},{32,28... | collective-permute-start | bytes 2359304 | tf_op jit(solution)/shard_map/ppermute | solution.py:866
  13.7 0.0 copy-done.10
  13.7 0.0 copy-done.9
  13.7 0.1 pad_add_fusion.refs_0_.whole_ref
  13.8 0.0 copy-done.12
  13.8 0.0 copy-done.11
  13.8 0.1 pad_maximum_fusion.refs_1_.real_ref
  13.9 0.0 copy-done.2
  13.9 0.0 copy-done.7
  13.9 0.0 copy-start.4
  13.9 0.9 %copy-done.4 = f32[16,2,2048]{2,1,0:T(2,128)S(1)} copy-done((f32[16,2,2048]{2,1,0:T(2,128)S(1)}, f32[16,2,2048]{2,1,0:T(2,128)}, u32[]{:S(2)}) %copy-start.4) | copy-done | bytes 262168
  14.9 9.3 %forward_inner.1 = (f32[22,2,16,2048]{3,2,1,0:T(8,128)S(1)}, f32[20,2,16,2048]{3,2,1,0:T(8,128)S(1)}, f32[18,2,16,2048]{3,2,1,0:T(8,128)S(1)}, f32[8,128]{1,0:T(...) custom-call(s32[33]{0:T(128)S(1)} %pad_add_fusion.refs_0_.whole_ref, ...), custom_call_target="tpu_custom_call" | custom-call | tf_op jit(solution)/shard_map/forward_inner/pallas_call | solution.py:590
  24.2 0.0 copy-start.3
  24.2 0.0 copy-start.5
  24.2 8.5 %adjoint_inner.1 = (f32[22,2,16,2048]{3,2,1,0:T(8,128)S(1)}, f32[20,2,16,2048]{3,2,1,0:T(8,128)S(1)}, f32[18,2,16,2048]{3,2,1,0:T(8,128)S(1)}, f32[8,128]{1,0:T(8,128)S(1)}) custom-call(s32[33]{0:T(128)S(1)} %pad_add_fusion.refs_0_.whole_ref, f32[48]{0:T(128)S(1)} %pad_maximum_fusion.refs_1_.real_ref, f32[16,2,16,2048]{3,2,1,0:T(8,128)S(1)} %copy-done, ...), custom_call_target="tpu_custom_call" | custom-call | tf_op jit(solution)/shard_map/adjoint_inner/pallas_call | solution.py:590
  32.7 0.0 collective-permute-done.2.refs_2_
  32.8 0.0 collective-permute-done.3.refs_3_
  32.8 0.0 copy-done.3
  32.8 0.0 copy-done.5
  32.8 5.2 %forward_outer.1 = (f32[22,2,16,2048]{3,2,1,0:T(8,128)S(1)}, f32[20,2,16,2048]{3,2,1,0:T(8,128)S(1)}, f32[18,2,16,2048]{3,2,1,0:T(8,128)S(1)}, f32[20,16,2048]{2...) custom-call(s32[33]{0:T(128)S(1)} %pad_add_fusion.refs_0_.whole_ref,, ...), custom_call_target="tpu_custom_call", output_to_operand_aliasing={{0}: (5, {}), {1}: (6, {}), {2}: (7, {}), {3}: (8, {}), {4}... | custom-call | tf_op jit(solution)/shard_map/forward_outer/pallas_call | solution.py:624
  38.0 3.7 %collective-permute-done.refs_2_ = f32[96,2048]{1,0:T(8,128)S(1)} collective-permute-done((f32[96,2048]{1,0:T(8,128)S(1)}, f32[96,2048]{1,0:T(8,128)S(1)}, u32[]{:S(2)}, u32[]{:S(2)}) %collective-permute-start) | collective-permute-done | bytes 786464 | tf_op jit(solution)/shard_map/ppermute | solution.py:865
  41.8 5.5 %collective-permute-done.1.refs_3_ = f32[96,2048]{1,0:T(8,128)S(1)} collective-permute-done((f32[96,2048]{1,0:T(8,128)S(1)}, f32[96,2048]{1,0:T(8,128)S(1)}, u32[]{:S(2)}, u32[]{:S(2)}) %collective-permute-start.1) | collective-permute-done | bytes 786464 | tf_op jit(solution)/shard_map/ppermute | solution.py:866
  47.3 6.4 %adjoint_outer.1 = (f32[22,2,16,2048]{3,2,1,0:T(8,128)S(1)}, f32[20,2,16,2048]{3,2,1,0:T(8,128)S(1)}, f32[18,2,16,2048]{3,2,1,0:T(8,128)S(1)}, f32[32,8,128]{2,1,0:T(8,128)S(1)}, f32[4,2,16,2048]{3,2,1,0:T(8,128)S(1)}) custom-call(s32[33]{0:T(128)S(1)} %pad_add_fusion.refs_0_.whole_ref, ...), custom_call_target="tpu_custom_call", output_to_operand_aliasing={{0}: (5, {}), {1}: (6, {}), {2}: (7, {})} | custom-call | tf_op jit(solution)/shard_map/adjoint_outer/pallas_call | solution.py:624
  53.7 15.5 %all_to_all.5.sums_ref = f32[32,8,128]{2,1,0:T(8,128)S(1)} all-to-all(f32[32,8,128]{2,1,0:T(8,128)S(1)} %get-tuple-element.48), channel_id=1, replica_groups=mesh['gx'=32,'wa'=4] {'gx'}, dimensions={0} | all-to-all | bytes 262144 | tf_op jit(solution)/shard_map/all_to_all | solution.py:896
  69.2 0.0 copy-start.8
  69.2 8.4 %finish.1 = (f32[16,2,16,2048]{3,2,1,0:T(8,128)}, f32[16,2,16,2048]{3,2,1,0:T(8,128)}, f32[16,2048]{1,0:T(8,128)S(1)}, f32[20,2,16,2048]{3,2,1,0:T(8,128)S(1)}, f32[18,2,16,2048]{3,2,1,0:T(8,128)S(1)}) custom-call(s32[33]{0:T(128)S(1)} %pad_add_fusion.refs_0_.whole_ref, ...), custom_call_target="tpu_custom_call", output_to_operand_aliasing={{3}: (7, {}), {4}: (8, {})} | custom-call | tf_op jit(solution)/shard_map/finish/pallas_call | solution.py:779
  77.6 10.9 %all-gather = f32[64,2048]{1,0:T(8,128)S(1)} all-gather(f32[16,2048]{1,0:T(8,128)S(1)} %get-tuple-element.58), channel_id=2, replica_groups=mesh['gx'=32,'wa'=4] {'wa'}, dimensions={0}, use_global_device_ids=true | all-gather | bytes 655360 | tf_op jit(solution)/shard_map/all_gather | solution.py:902
  88.5 0.0 copy-done.8
  88.5 0.7 convert_multiply_fusion
  (2 shorter events, 0.1 us)
Async XLA Ops:
  0.6 13.1 %copy-start.10 = (s32[16]{0:T(128)S(1)}, s32[16]{0:T(128)}, u32[]{:S(2)}) copy-start(s32[16]{0:T(128)} %param.14) | copy-start | bytes 196
  0.6 13.1 %copy-start.9 = (s32[16]{0:T(128)S(1)}, s32[16]{0:T(128)}, u32[]{:S(2)}) copy-start(s32[16]{0:T(128)} %param.15) | copy-start | bytes 196
  0.7 13.1 %copy-start.12 = (f32[16]{0:T(128)S(1)}, f32[16]{0:T(128)}, u32[]{:S(2)}) copy-start(f32[16]{0:T(128)} %param.17) | copy-start | bytes 196
  0.7 13.2 %copy-start.11 = (f32[16]{0:T(128)S(1)}, f32[16]{0:T(128)}, u32[]{:S(2)}) copy-start(f32[16]{0:T(128)} %param.16) | copy-start | bytes 196
  0.7 11.6 %copy-start = (f32[16,2,16,2048]{3,2,1,0:T(8,128)S(1)}, f32[16,2,16,2048]{3,2,1,0:T(8,128)}, u32[]{:S(2)}) copy-start(f32[16,2,16,2048]{3,2,1,0:T(8,128)} %refs_2_.3) | copy-start | bytes 12582916
  0.7 2.3 %copy-start.1 = (f32[16,2,16,2048]{3,2,1,0:T(8,128)S(1)}, f32[16,2,16,2048]{3,2,1,0:T(8,128)}, u32[]{:S(2)}) copy-start(f32[16,2,16,2048]{3,2,1,0:T(8,128)} %field_ref.3) | copy-start | bytes 12582916
  3.0 1.1 %copy-start.6 = (f32[16,2048]{1,0:T(8,128)S(1)}, f32[16,2048]{1,0:T(8,128)}, u32[]{:S(2)}) copy-start(f32[16,2048]{1,0:T(8,128)} %refs_0_.1) | copy-start | bytes 393220
  4.1 9.8 %copy-start.2 = (f32[16,2,16,2048]{3,2,1,0:T(8,128)S(1)}, f32[16,2,16,2048]{3,2,1,0:T(8,128)}, u32[]{:S(2)}) copy-start(f32[16,2,16,2048]{3,2,1,0:T(8,128)} %field_ref.3) | copy-start | bytes 12582916
  4.1 9.8 %copy-start.7 = (f32[16,2048]{1,0:T(8,128)S(1)}, f32[16,2048]{1,0:T(8,128)}, u32[]{:S(2)}) copy-start(f32[16,2048]{1,0:T(8,128)} %refs_0_.1) | copy-start | bytes 393220
  4.6 28.2 %collective-permute-start.2 = (f32[104,2048]{1,0:T(8,128)S(1)}, f32[104,2048]{1,0:T(8,128)S(1)}, u32[]{:S(2)}, u32[]{:S(2)}) collective-permute-start(f32[104,2048]{1,0:T(8,128)S(1)} %get-tuple-element.39), channel_id=1, source_target_pairs={{0,4},{4,0},{8,12},{12,8},{16,20},{20,16},{24,28},{28,24},{32,36},... | collective-permute-start | bytes 2555912 | tf_op jit(solution)/shard_map/ppermute | solution.py:860
  6.7 26.1 %collective-permute-start.3 = (f32[104,2048]{1,0:T(8,128)S(1)}, f32[104,2048]{1,0:T(8,128)S(1)}, u32[]{:S(2)}, u32[]{:S(2)}) collective-permute-start(f32[104,2048]{1,0:T(8,128)S(1)} %get-tuple-element.40), channel_id=1, source_target_pairs={{0,124},{4,8},{8,4},{12,16},{16,12},{20,24},{24,20},{28,32},{32,28... | collective-permute-start | bytes 2555912 | tf_op jit(solution)/shard_map/ppermute | solution.py:861
  12.7 29.1 %collective-permute-start = (f32[96,2048]{1,0:T(8,128)S(1)}, f32[96,2048]{1,0:T(8,128)S(1)}, u32[]{:S(2)}, u32[]{:S(2)}) collective-permute-start(f32[96,2048]{1,0:T(8,128)S(1)} %get-tuple-element.31), channel_id=1, source_target_pairs={{0,4},{4,0},{8,12},{12,8},{16,20},{20,16},{24,28},{28,24},{32,36},... | collective-permute-start | bytes 2359304 | tf_op jit(solution)/shard_map/ppermute | solution.py:865
  12.8 34.5 %collective-permute-start.1 = (f32[96,2048]{1,0:T(8,128)S(1)}, f32[96,2048]{1,0:T(8,128)S(1)}, u32[]{:S(2)}, u32[]{:S(2)}) collective-permute-start(f32[96,2048]{1,0:T(8,128)S(1)} %get-tuple-element.32), channel_id=1, source_target_pairs={{0,124},{4,8},{8,4},{12,16},{16,12},{20,24},{24,20},{28,32},{32,28... | collective-permute-start | bytes 2359304 | tf_op jit(solution)/shard_map/ppermute | solution.py:866
  13.9 1.0 %copy-start.4 = (f32[16,2,2048]{2,1,0:T(2,128)S(1)}, f32[16,2,2048]{2,1,0:T(2,128)}, u32[]{:S(2)}) copy-start(f32[16,2,2048]{2,1,0:T(2,128)} %refs_10_.2) | copy-start | bytes 786436
  24.2 8.6 %copy-start.3 = (f32[16,2,2048]{2,1,0:T(2,128)S(1)}, f32[16,2,2048]{2,1,0:T(2,128)}, u32[]{:S(2)}) copy-start(f32[16,2,2048]{2,1,0:T(2,128)} %refs_10_.3) | copy-start | bytes 786436
  24.2 8.6 %copy-start.5 = (f32[16,2,2048]{2,1,0:T(2,128)S(1)}, f32[16,2,2048]{2,1,0:T(2,128)}, u32[]{:S(2)}) copy-start(f32[16,2,2048]{2,1,0:T(2,128)} %refs_10_.2) | copy-start | bytes 786436
  69.2 19.3 %copy-start.8 = (s32[16,2048]{1,0:T(8,128)S(1)}, s32[16,2048]{1,0:T(8,128)}, u32[]{:S(2)}) copy-start(s32[16,2048]{1,0:T(8,128)} %param.13) | copy-start | bytes 393220

commit v2 on v1

--- a/solution.py
+++ b/solution.py
@@ -130,8 +130,8 @@
     def __init__(self, x_ref, z_ref, u_ref, diag_ref, inv_ref, wave_ref):
         self.x, self.z, self.u = x_ref, z_ref, u_ref
         self.diag, self.inv, self.wave = diag_ref, inv_ref, wave_ref
-        _, self.parts, self.waves, width = x_ref.shape
-        self.rows = x_ref.shape[0] - 2 * HALO
+        _, self.parts, self.waves, width = z_ref.shape
+        self.rows = z_ref.shape[0] - 4
         self.tiles = width // LANES
 
     def groups(self):
@@ -352,8 +352,8 @@
         (part_ref, _, _, _, _, _, side_ref, mark_ref) = refs[:8]
         (x_ref, z_ref, u_ref, diag_ref, inv_ref, sums_ref, table_ref, mark_sums) = refs[8:]
     else:
-        (part_ref, _, _, _, diag_ref, inv_ref, mark_ref, fwd_sums_ref) = refs[:8]
-        (x_ref, z_ref, u_ref, sums_ref, line_ref, table_ref, line_sums, g_ref) = refs[8:]
+        (part_ref, _, _, _, diag_ref, inv_ref, line_ref, inner_line_sums, fwd_sums_ref) = refs[:9]
+        (x_ref, z_ref, u_ref, sums_ref, table_ref, line_sums) = refs[9:]
     step = Rows(x_ref, z_ref, u_ref, diag_ref, inv_ref, table_ref)
     rows, parts, waves, tiles = step.rows, step.parts, step.waves, step.tiles
     first_row = scalars.first_row
@@ -440,7 +440,18 @@
         lax.fori_loop(0, rows, mark_at, 0)
         extra, count = mark_sums, MARK_SUMS
     else:
-        line_terms(step, scalars, total_rows, mark_ref, line_ref, line_sums, g_ref)
+        line_products(
+            step,
+            scalars,
+            total_rows,
+            line_ref,
+            line_sums,
+            lambda row: jnp.logical_and(
+                jnp.logical_and(row >= 0, row < rows),
+                jnp.logical_or(row < 3, row >= rows - 3),
+            ),
+        )
+        line_sums[...] += inner_line_sums[...]
         extra, count = line_sums, LINE_SUMS
     out = part_ref[...]
     new = jnp.zeros((SUBLANES, LANES), jnp.float32)
@@ -466,110 +477,155 @@
     return a[0] * b[0] + a[1] * b[1], a[0] * b[1] - a[1] * b[0]
 
 
-def line_terms(step, scalars, total_rows, mark_ref, line_ref, line_sums, g_ref):
+def line_waves(step, scalars, total_rows, body):
+    def one_wave(w, _):
+        away = distance_to(scalars.monitor(w), scalars.first_row, total_rows)
+
+        @pl.when(away <= step.rows + 1)
+        def _():
+            group = pl.ds(pl.multiple_of((w // SUBLANES) * SUBLANES, SUBLANES), SUBLANES)
+            sublane = lax.broadcasted_iota(jnp.int32, (SUBLANES, LANES), 0)
+            body(away, group, sublane == w % SUBLANES)
+
+        return 0
+
+    lax.fori_loop(0, step.waves, one_wave, 0)
+
+
+def line_plane(line_ref, n, part, group, mine):
+    return lambda j: jnp.where(mine, line_ref[n, part, group, lane_slice(j)], 0.0)
+
+
+def line_fields(step, scalars, total_rows, mark_ref, line_ref):
     rows, tiles = step.rows, step.tiles
     line_ref[...] = jnp.zeros_like(line_ref)
+
+    def body(away, group, mine):
+        cosine, sine = step.frame(away, group)
+        before = jnp.maximum(away + 1, 0)
+        after = jnp.minimum(away + 3, rows + 3)
+        for j in range(tiles):
+            lanes = lane_slice(j)
+            m_re = jnp.where(mine, mark_ref[group, 0, lanes], 0.0)
+            m_im = jnp.where(mine, mark_ref[group, 1, lanes], 0.0)
+            g = (cosine * m_re + sine * m_im, sine * m_re - cosine * m_im)
+            for part in range(2):
+                z = g[part] * step.inv[away + 2, group, lanes]
+                line_ref[0, part, group, lanes] += z
+                line_ref[1, part, group, lanes] -= z * step.inv[before, group, lanes]
+                line_ref[3, part, group, lanes] -= z * step.inv[after, group, lanes]
+                line_ref[4, part, group, lanes] += g[part]
+        for part in range(2):
+            for j, _, sides in lane_neighbours(line_plane(line_ref, 0, part, group, mine), tiles):
+                lanes = lane_slice(j)
+                image = line_plane(line_ref, 4, part, group, mine)(j) - sides
+                line_ref[5, part, group, lanes] += image
+                line_ref[2, part, group, lanes] += image * step.inv[away + 2, group, lanes]
+
+    line_waves(step, scalars, total_rows, body)
+
+
+def line_products(step, scalars, total_rows, line_ref, line_sums, counts):
     line_sums[...] = jnp.zeros_like(line_sums)
-    sublane = lax.broadcasted_iota(jnp.int32, (SUBLANES, LANES), 0)
-
-    def one_wave(w, _):
-        away = distance_to(scalars.monitor(w), scalars.first_row, total_rows)
-
-        @pl.when(away <= rows + 1)
-        def _():
-            group = pl.ds(pl.multiple_of((w // SUBLANES) * SUBLANES, SUBLANES), SUBLANES)
-            mine = sublane == w % SUBLANES
-            cosine, sine = step.frame(away, group)
-            before = jnp.maximum(away + 1, 0)
-            after = jnp.minimum(away + 3, rows + 3)
-            for j in range(tiles):
-                lanes = lane_slice(j)
-                m_re = jnp.where(mine, mark_ref[group, 0, lanes], 0.0)
-                m_im = jnp.where(mine, mark_ref[group, 1, lanes], 0.0)
-                g = (cosine * m_re + sine * m_im, sine * m_re - cosine * m_im)
-                inverse = step.inv[away + 2, group, lanes]
-                for part in range(2):
-                    z = g[part] * inverse
-                    g_ref[0, part, :, lanes] = g[part]
-                    g_ref[1, part, :, lanes] = z
-                    g_ref[2, part, :, lanes] = -z * step.inv[before, group, lanes]
-                    g_ref[4, part, :, lanes] = -z * step.inv[after, group, lanes]
-            for part in range(2):
-                for j, _, sides in lane_neighbours(
-                    lambda j, part=part: g_ref[1, part, :, lane_slice(j)], tiles
-                ):
-                    lanes = lane_slice(j)
-                    image = g_ref[0, part, :, lanes] - sides
-                    g_ref[5, part, :, lanes] = image
-                    g_ref[3, part, :, lanes] = image * step.inv[away + 2, group, lanes]
-            for part in range(2):
-                for j in range(tiles):
-                    lanes = lane_slice(j)
-                    for n in range(4):
-                        line_ref[n, part, group, lanes] += g_ref[n + 1, part, :, lanes]
-            for k in range(-2, 3):
-
-                @pl.when(jnp.logical_and(away + k >= 0, away + k < rows))
-                def _(k=k):
-                    zero = jnp.zeros((SUBLANES, LANES), jnp.float32)
-                    totals = [zero] * LINE_SUMS
-
-                    def add(at, pair):
-                        totals[at] = totals[at] + pair[0]
-                        totals[at + 1] = totals[at + 1] + pair[1]
-
+
+    def body(away, group, mine):
+        for k in range(-2, 3):
+
+            @pl.when(counts(away + k))
+            def _(k=k):
+                zero = jnp.zeros((SUBLANES, LANES), jnp.float32)
+                totals = [zero] * LINE_SUMS
+
+                def add(at, pair):
+                    totals[at] = totals[at] + pair[0]
+                    totals[at + 1] = totals[at + 1] + pair[1]
+
+                if abs(k) < 2:
+                    sides_of = [
+                        [
+                            sides
+                            for _, _, sides in lane_neighbours(
+                                line_plane(line_ref, 2 + k, part, group, mine), step.tiles
+                            )
+                        ]
+                        for part in range(2)
+                    ]
+                for j, r, v, w_vec in step.vectors(away + k, group):
+                    get = lambda n: [
+                        line_plane(line_ref, n, part, group, mine)(j) for part in range(2)
+                    ]
+                    if abs(k) == 2:
+                        wg = [-t for t in get(1 if k < 0 else 3)]
+                    elif abs(k) == 1:
+                        vg = [-t for t in get(0)]
+                        mid = get(2)
+                        wg = [vg[p] - mid[p] - sides_of[p][j] for p in range(2)]
+                    else:
+                        g, vg, low, high = get(4), get(5), get(1), get(3)
+                        wg = [vg[p] - (low[p] + high[p]) - sides_of[p][j] for p in range(2)]
+                    add(0, dot(wg, r))
+                    add(2, dot(wg, v))
+                    add(4, dot(w_vec, wg))
+                    totals[6] = totals[6] + dot(wg, wg)[0]
                     if abs(k) < 2:
-                        sides_of = [
-                            [
-                                sides
-                                for _, _, sides in lane_neighbours(
-                                    lambda j, part=part: g_ref[3 + k, part, :, lane_slice(j)],
-                                    tiles,
-                                )
-                            ]
-                            for part in range(2)
-                        ]
-                    for j, r, v, w_vec in step.vectors(away + k, group):
-                        lanes = lane_slice(j)
-                        get = lambda n: [g_ref[n, part, :, lanes] for part in range(2)]
-                        r = [jnp.where(mine, t, 0.0) for t in r]
-                        v = [jnp.where(mine, t, 0.0) for t in v]
-                        w_vec = [jnp.where(mine, t, 0.0) for t in w_vec]
-                        if abs(k) == 2:
-                            wg = [-t for t in get(2 if k < 0 else 4)]
-                        elif abs(k) == 1:
-                            vg = [-t for t in get(1)]
-                            mid = get(3)
-                            wg = [vg[p] - mid[p] - sides_of[p][j] for p in range(2)]
-                        else:
-                            g, vg, low, high = get(0), get(5), get(2), get(4)
-                            wg = [
-                                vg[p] - (low[p] + high[p]) - sides_of[p][j] for p in range(2)
-                            ]
-                        add(0, dot(wg, r))
-                        add(2, dot(wg, v))
-                        add(4, dot(w_vec, wg))
-                        totals[6] = totals[6] + dot(wg, wg)[0]
-                        if abs(k) < 2:
-                            add(7, dot(r, vg))
-                            add(9, dot(v, vg))
-                            add(11, dot(w_vec, vg))
-                            add(13, dot(wg, vg))
-                            totals[15] = totals[15] + dot(vg, vg)[0]
-                        if k == 0:
-                            add(16, dot(r, g))
-                            add(18, dot(g, v))
-                            add(20, dot(g, vg))
-                            add(22, dot(w_vec, g))
-                            add(24, dot(wg, g))
-                            totals[26] = totals[26] + dot(g, g)[0]
-                    used = 7 if abs(k) == 2 else 16 if abs(k) == 1 else LINE_SUMS
-                    for n in range(used):
-                        line_sums[n, group] += totals[n]
-
-        return 0
-
-    lax.fori_loop(0, step.waves, one_wave, 0)
+                        add(7, dot(r, vg))
+                        add(9, dot(v, vg))
+                        add(11, dot(w_vec, vg))
+                        add(13, dot(wg, vg))
+                        totals[15] = totals[15] + dot(vg, vg)[0]
+                    if k == 0:
+                        add(16, dot(r, g))
+                        add(18, dot(g, v))
+                        add(20, dot(g, vg))
+                        add(22, dot(w_vec, g))
+                        add(24, dot(wg, g))
+                        totals[26] = totals[26] + dot(g, g)[0]
+                used = 7 if abs(k) == 2 else 16 if abs(k) == 1 else LINE_SUMS
+                for n in range(used):
+                    line_sums[n, group] += totals[n]
+
+    line_waves(step, scalars, total_rows, body)
+
+
+def line_kernel(
+    whole_ref,
+    real_ref,
+    z_ref,
+    u_ref,
+    diag_ref,
+    inv_ref,
+    mark_ref,
+    line_ref,
+    line_sums,
+    table_ref,
+    *,
+    total_rows,
+):
+    scalars = Scalars(whole_ref, real_ref)
+    step = Rows(None, z_ref, u_ref, diag_ref, inv_ref, table_ref)
+    fill_table(table_ref, scalars, step.rows, total_rows, -1.0)
+    line_fields(step, scalars, total_rows, mark_ref, line_ref)
+    line_products(
+        step,
+        scalars,
+        total_rows,
+        line_ref,
+        line_sums,
+        lambda row: jnp.logical_and(row >= 3, row < step.rows - 3),
+    )
+
+
+def inner_lines(scalars, z, u, diag, inv, profile, total_rows):
+    _, parts, waves, width = z.shape
+    return pl.pallas_call(
+        functools.partial(line_kernel, total_rows=total_rows),
+        in_specs=[SMEM] * 2 + [VMEM] * 5,
+        out_specs=[VMEM, VMEM],
+        out_shape=[array(6, parts, waves, width), array(LINE_SUMS, waves, LANES)],
+        scratch_shapes=[pltpu.VMEM((TABLE_COLUMNS, waves, LANES), jnp.float32)],
+        compiler_params=pltpu.CompilerParams(vmem_limit_bytes=INNER_LIMIT),
+        name="adjoint_line",
+    )(*scalars, z, u, diag, inv, profile)
 
 
 def array(*shape):
@@ -612,15 +668,9 @@
         aliases = {5: 0, 6: 1, 7: 2, 8: 3, 9: 4}
         scratch += [pltpu.VMEM((MARK_SUMS, waves, LANES), jnp.float32)]
     else:
-        out_shape = [array(*a.shape) for a in (x, z, u)] + [
-            array(copies, SUBLANES, LANES),
-            array(4, 2, waves, x.shape[-1]),
-        ]
+        out_shape = [array(*a.shape) for a in (x, z, u)] + [array(copies, SUBLANES, LANES)]
         aliases = {5: 0, 6: 1, 7: 2}
-        scratch += [
-            pltpu.VMEM((LINE_SUMS, waves, LANES), jnp.float32),
-            pltpu.VMEM((6, 2, SUBLANES, x.shape[-1]), jnp.float32),
-        ]
+        scratch += [pltpu.VMEM((LINE_SUMS, waves, LANES), jnp.float32)]
     return pl.pallas_call(
         functools.partial(outer_kernel, forward=forward, total_rows=total_rows),
         in_specs=[SMEM] * 2 + [VMEM] * (len(args) - 2),
@@ -882,12 +932,13 @@
         count,
         total_rows,
     )
-    ax, az, au, sums, line = outer_rows_solve(
+    line, line_sums = inner_lines(scalars, az, au, diag, inv, monitor_profile, total_rows)
+    ax, az, au, sums = outer_rows_solve(
         False,
         scalars,
         adj_got,
         (ax, az, au, a_sums, diag, inv),
-        (monitor_profile, f_sums),
+        (line, line_sums, f_sums),
         count,
         total_rows,
     )

time: 90.4 us -> 88.8 us (0.982)
  waiting for transfers between devices: 9.27 us -> 7.54 us
  Pallas kernels: 38.7 us -> 40.1 us
  blocking collectives: 26.4 us -> 25.2 us
    pallas_call x0 -> x1, Pallas kernels: none -> 2.09 us  [inner_lines(): pl.pallas_call(functools.partial(line_kernel, total_rows=total_rows), in_...]
    ppermute x1, waiting for transfers between devices: 3.73 us -> 2 us  [local(): lax.ppermute(adj_first, 'gx', pairing_one)]
  transfers between devices with their start and end apart: 4 -> 4, of which waited for: 2 -> 2; matrix products, arithmetic and copies ran while one was open for 0% -> 0% of each run, Pallas kernels for 26% -> 29%
where the time goes in v2:
time: 88.8 us; the launch traced here: 87.7 us
  Pallas kernels  40.1 us (45%)
  blocking collectives  25.2 us (28%)
  starting transfers between devices  8.72 us (10%)
  waiting for transfers between devices  7.54 us (8%)
  local copies, waits for them, and re-layouts  4.46 us (5%)
    pallas_call x2, Pallas kernels, inner_rows(): pl.pallas_call(functools.partial(inner_kernel, forward=forward, total_row...  17.5 us
    all_to_all x1, blocking collectives, local(): lax.all_to_all(sums, 'gx', 0, 0, tiled=True)  15.2 us
    pallas_call x2, Pallas kernels, outer_rows_solve(): pl.pallas_call(functools.partial(outer_kernel, forward=forward, total_row...  11.2 us
    all_gather x1, blocking collectives, local(): summed_terms = lax.all_gather(partial, 'wa').sum(axis=0)  10 us
    pallas_call x1, Pallas kernels, finish(): pl.pallas_call(functools.partial(finish_kernel, total_rows=total_rows), i...  8.47 us
    ppermute x1, starting transfers between devices, local(): lax.ppermute(fwd_second, 'gx', pairing_two)  5.62 us
    ppermute x1, waiting for transfers between devices, local(): lax.ppermute(adj_second, 'gx', pairing_two)  5.54 us
    unnamed x26, local copies, waits for them, and re-layouts  4.42 us
  transfers between devices with their start and end apart: 4, of which 2 were waited for; matrix products, arithmetic and copies ran while one was open for 0% of the time, Pallas kernels for 29%

profile of v2, /device:TPU:1, one launch (start us, length us, event | category | flops | bytes accessed | tf_op | source)
XLA Modules:
  0.0 87.7 jit_solution(3377428447136155000)
XLA Ops:
  0.6 0.0 copy-start.10
  0.6 0.0 copy-start.9
  0.7 0.0 copy-start.12
  0.7 0.0 copy-start.11
  0.7 0.0 copy-start
  0.7 0.0 copy-start.1
  0.7 2.3 %copy-done.1 = f32[16,2,16,2048]{3,2,1,0:T(8,128)S(1)} copy-done((f32[16,2,16,2048]{3,2,1,0:T(8,128)S(1)}, f32[16,2,16,2048]{3,2,1,0:T(8,128)}, u32[]{:S(2)}) %copy-start.1) | copy-done | bytes 4194328
  3.0 0.0 copy-start.6
  3.0 1.1 %copy-done.6 = f32[16,2048]{1,0:T(8,128)S(1)} copy-done((f32[16,2048]{1,0:T(8,128)S(1)}, f32[16,2048]{1,0:T(8,128)}, u32[]{:S(2)}) %copy-start.6) | copy-done | bytes 131096
  4.1 0.0 copy-start.2
  4.1 0.0 copy-start.7
  4.1 0.4 outer_rows.3
  4.6 2.1 %collective-permute-start.2 = (f32[104,2048]{1,0:T(8,128)S(1)}, f32[104,2048]{1,0:T(8,128)S(1)}, u32[]{:S(2)}, u32[]{:S(2)}) collective-permute-start(f32[104,2048]{1,0:T(8,128)S(1)} %get-tuple-element.40), channel_id=1, source_target_pairs={{0,4},{4,0},{8,12},{12,8},{16,20},{20,16},{24,28},{28,24},{32,36},... | collective-permute-start | bytes 2555912 | tf_op jit(solution)/shard_map/ppermute | solution.py:910
  6.7 5.6 %collective-permute-start.3 = (f32[104,2048]{1,0:T(8,128)S(1)}, f32[104,2048]{1,0:T(8,128)S(1)}, u32[]{:S(2)}, u32[]{:S(2)}) collective-permute-start(f32[104,2048]{1,0:T(8,128)S(1)} %get-tuple-element.41), channel_id=1, source_target_pairs={{0,124},{4,8},{8,4},{12,16},{16,12},{20,24},{24,20},{28,32},{32,28... | collective-permute-start | bytes 2555912 | tf_op jit(solution)/shard_map/ppermute | solution.py:911
  12.3 0.0 copy-done
  12.3 0.4 outer_rows.2
  12.7 0.1 collective-permute-start
  12.8 0.9 %collective-permute-start.1 = (f32[96,2048]{1,0:T(8,128)S(1)}, f32[96,2048]{1,0:T(8,128)S(1)}, u32[]{:S(2)}, u32[]{:S(2)}) collective-permute-start(f32[96,2048]{1,0:T(8,128)S(1)} %get-tuple-element.33), channel_id=1, source_target_pairs={{0,124},{4,8},{8,4},{12,16},{16,12},{20,24},{24,20},{28,32},{32,28... | collective-permute-start | bytes 2359304 | tf_op jit(solution)/shard_map/ppermute | solution.py:916
  13.7 0.0 copy-done.10
  13.7 0.0 copy-done.9
  13.7 0.1 pad_add_fusion.refs_0_.whole_ref
  13.8 0.0 copy-done.12
  13.8 0.0 copy-done.11
  13.8 0.1 pad_maximum_fusion.refs_1_.real_ref
  13.9 0.0 copy-done.2
  13.9 0.0 copy-done.7
  13.9 0.0 copy-start.4
  13.9 0.9 %copy-done.4 = f32[16,2,2048]{2,1,0:T(2,128)S(1)} copy-done((f32[16,2,2048]{2,1,0:T(2,128)S(1)}, f32[16,2,2048]{2,1,0:T(2,128)}, u32[]{:S(2)}) %copy-start.4) | copy-done | bytes 262168
  14.9 9.0 %forward_inner.1 = (f32[22,2,16,2048]{3,2,1,0:T(8,128)S(1)}, f32[20,2,16,2048]{3,2,1,0:T(8,128)S(1)}, f32[18,2,16,2048]{3,2,1,0:T(8,128)S(1)}, f32[8,128]{1,0:T(...) custom-call(s32[33]{0:T(128)S(1)} %pad_add_fusion.refs_0_.whole_ref, ...), custom_call_target="tpu_custom_call" | custom-call | tf_op jit(solution)/shard_map/forward_inner/pallas_call | solution.py:646
  23.9 0.0 copy-start.3
  23.9 0.0 copy-start.5
  23.9 8.5 %adjoint_inner.1 = (f32[22,2,16,2048]{3,2,1,0:T(8,128)S(1)}, f32[20,2,16,2048]{3,2,1,0:T(8,128)S(1)}, f32[18,2,16,2048]{3,2,1,0:T(8,128)S(1)}, f32[8,128]{1,0:T(8,128)S(1)}) custom-call(s32[33]{0:T(128)S(1)} %pad_add_fusion.refs_0_.whole_ref, f32[48]{0:T(128)S(1)} %pad_maximum_fusion.refs_1_.real_ref, f32[16,2,16,2048]{3,2,1,0:T(8,128)S(1)} %copy-done, ...), custom_call_target="tpu_custom_call" | custom-call | tf_op jit(solution)/shard_map/adjoint_inner/pallas_call | solution.py:646
  32.4 0.0 collective-permute-done.2.refs_2_
  32.4 0.0 collective-permute-done.3.refs_3_
  32.4 0.0 copy-done.3
  32.5 0.0 copy-done.5
  32.5 5.2 %forward_outer.1 = (f32[22,2,16,2048]{3,2,1,0:T(8,128)S(1)}, f32[20,2,16,2048]{3,2,1,0:T(8,128)S(1)}, f32[18,2,16,2048]{3,2,1,0:T(8,128)S(1)}, f32[20,16,2048]{2...) custom-call(s32[33]{0:T(128)S(1)} %pad_add_fusion.refs_0_.whole_ref,, ...), custom_call_target="tpu_custom_call", output_to_operand_aliasing={{0}: (5, {}), {1}: (6, {}), {2}: (7, {}), {3}: (8, {}), {4}... | custom-call | tf_op jit(solution)/shard_map/forward_outer/pallas_call | solution.py:674
  37.7 2.1 %adjoint_line.1 = (f32[6,2,16,2048]{3,2,1,0:T(8,128)S(1)}, f32[27,16,128]{2,1,0:T(8,128)S(1)}) custom-call(s32[33]{0:T(128)S(1)} %pad_add_fusion.refs_0_.whole_ref, f32[48]{0:T(128)S(1)} %pad_maximum_fusion.refs_1_.real_ref, f32[20,2,16,2048]{3,2,1,0:T(8,128)S(1)} %get-tuple-element.38.z_ref.refs_6_, ...), custom_call_target="tpu_custom_call" | custom-call | tf_op jit(solution)/shard_map/adjoint_line/pallas_call | solution.py:620
  39.8 2.0 %collective-permute-done.refs_2_ = f32[96,2048]{1,0:T(8,128)S(1)} collective-permute-done((f32[96,2048]{1,0:T(8,128)S(1)}, f32[96,2048]{1,0:T(8,128)S(1)}, u32[]{:S(2)}, u32[]{:S(2)}) %collective-permute-start) | collective-permute-done | bytes 786464 | tf_op jit(solution)/shard_map/ppermute | solution.py:915
  41.8 5.5 %collective-permute-done.1.refs_3_ = f32[96,2048]{1,0:T(8,128)S(1)} collective-permute-done((f32[96,2048]{1,0:T(8,128)S(1)}, f32[96,2048]{1,0:T(8,128)S(1)}, u32[]{:S(2)}, u32[]{:S(2)}) %collective-permute-start.1) | collective-permute-done | bytes 786464 | tf_op jit(solution)/shard_map/ppermute | solution.py:916
  47.3 6.0 %adjoint_outer.1 = (f32[22,2,16,2048]{3,2,1,0:T(8,128)S(1)}, f32[20,2,16,2048]{3,2,1,0:T(8,128)S(1)}, f32[18,2,16,2048]{3,2,1,0:T(8,128)S(1)}, f32[32,8,128]{2,1,0:T(8,128)S(1)}) custom-call(s32[33]{0:T(128)S(1)} %pad_add_fusion.refs_0_.whole_ref, ...), custom_call_target="tpu_custom_call", output_to_operand_aliasing={{0}: (5, {}), {1}: (6, {}), {2}: (7, {})} | custom-call | tf_op jit(solution)/shard_map/adjoint_outer/pallas_call | solution.py:674
  53.3 15.2 %all_to_all.5.sums_ref = f32[32,8,128]{2,1,0:T(8,128)S(1)} all-to-all(f32[32,8,128]{2,1,0:T(8,128)S(1)} %get-tuple-element.51), channel_id=1, replica_groups=mesh['gx'=32,'wa'=4] {'gx'}, dimensions={0} | all-to-all | bytes 262144 | tf_op jit(solution)/shard_map/all_to_all | solution.py:947
  68.5 0.0 copy-start.8
  68.5 8.5 %finish.1 = (f32[16,2,16,2048]{3,2,1,0:T(8,128)}, f32[16,2,16,2048]{3,2,1,0:T(8,128)}, f32[16,2048]{1,0:T(8,128)S(1)}, f32[20,2,16,2048]{3,2,1,0:T(8,128)S(1)}, f32[18,2,16,2048]{3,2,1,0:T(8,128)S(1)}) custom-call(s32[33]{0:T(128)S(1)} %pad_add_fusion.refs_0_.whole_ref, ...), custom_call_target="tpu_custom_call", output_to_operand_aliasing={{3}: (7, {}), {4}: (8, {})} | custom-call | tf_op jit(solution)/shard_map/finish/pallas_call | solution.py:829
  77.0 10.0 %all-gather = f32[64,2048]{1,0:T(8,128)S(1)} all-gather(f32[16,2048]{1,0:T(8,128)S(1)} %get-tuple-element.60), channel_id=2, replica_groups=mesh['gx'=32,'wa'=4] {'wa'}, dimensions={0}, use_global_device_ids=true | all-gather | bytes 655360 | tf_op jit(solution)/shard_map/all_gather | solution.py:953
  87.1 0.0 copy-done.8
  87.1 0.7 convert_multiply_fusion
  (2 shorter events, 0.1 us)
Async XLA Ops:
  0.6 13.1 %copy-start.10 = (s32[16]{0:T(128)S(1)}, s32[16]{0:T(128)}, u32[]{:S(2)}) copy-start(s32[16]{0:T(128)} %param.14) | copy-start | bytes 196
  0.6 13.1 %copy-start.9 = (s32[16]{0:T(128)S(1)}, s32[16]{0:T(128)}, u32[]{:S(2)}) copy-start(s32[16]{0:T(128)} %param.15) | copy-start | bytes 196
  0.7 13.1 %copy-start.12 = (f32[16]{0:T(128)S(1)}, f32[16]{0:T(128)}, u32[]{:S(2)}) copy-start(f32[16]{0:T(128)} %param.17) | copy-start | bytes 196
  0.7 13.2 %copy-start.11 = (f32[16]{0:T(128)S(1)}, f32[16]{0:T(128)}, u32[]{:S(2)}) copy-start(f32[16]{0:T(128)} %param.16) | copy-start | bytes 196
  0.7 11.6 %copy-start = (f32[16,2,16,2048]{3,2,1,0:T(8,128)S(1)}, f32[16,2,16,2048]{3,2,1,0:T(8,128)}, u32[]{:S(2)}) copy-start(f32[16,2,16,2048]{3,2,1,0:T(8,128)} %refs_2_.3) | copy-start | bytes 12582916
  0.7 2.3 %copy-start.1 = (f32[16,2,16,2048]{3,2,1,0:T(8,128)S(1)}, f32[16,2,16,2048]{3,2,1,0:T(8,128)}, u32[]{:S(2)}) copy-start(f32[16,2,16,2048]{3,2,1,0:T(8,128)} %field_ref.3) | copy-start | bytes 12582916
  3.0 1.1 %copy-start.6 = (f32[16,2048]{1,0:T(8,128)S(1)}, f32[16,2048]{1,0:T(8,128)}, u32[]{:S(2)}) copy-start(f32[16,2048]{1,0:T(8,128)} %refs_0_.1) | copy-start | bytes 393220
  4.1 9.8 %copy-start.2 = (f32[16,2,16,2048]{3,2,1,0:T(8,128)S(1)}, f32[16,2,16,2048]{3,2,1,0:T(8,128)}, u32[]{:S(2)}) copy-start(f32[16,2,16,2048]{3,2,1,0:T(8,128)} %field_ref.3) | copy-start | bytes 12582916
  4.1 9.8 %copy-start.7 = (f32[16,2048]{1,0:T(8,128)S(1)}, f32[16,2048]{1,0:T(8,128)}, u32[]{:S(2)}) copy-start(f32[16,2048]{1,0:T(8,128)} %refs_0_.1) | copy-start | bytes 393220
  4.6 27.9 %collective-permute-start.2 = (f32[104,2048]{1,0:T(8,128)S(1)}, f32[104,2048]{1,0:T(8,128)S(1)}, u32[]{:S(2)}, u32[]{:S(2)}) collective-permute-start(f32[104,2048]{1,0:T(8,128)S(1)} %get-tuple-element.40), channel_id=1, source_target_pairs={{0,4},{4,0},{8,12},{12,8},{16,20},{20,16},{24,28},{28,24},{32,36},... | collective-permute-start | bytes 2555912 | tf_op jit(solution)/shard_map/ppermute | solution.py:910
  6.7 25.8 %collective-permute-start.3 = (f32[104,2048]{1,0:T(8,128)S(1)}, f32[104,2048]{1,0:T(8,128)S(1)}, u32[]{:S(2)}, u32[]{:S(2)}) collective-permute-start(f32[104,2048]{1,0:T(8,128)S(1)} %get-tuple-element.41), channel_id=1, source_target_pairs={{0,124},{4,8},{8,4},{12,16},{16,12},{20,24},{24,20},{28,32},{32,28... | collective-permute-start | bytes 2555912 | tf_op jit(solution)/shard_map/ppermute | solution.py:911
  12.7 29.1 %collective-permute-start = (f32[96,2048]{1,0:T(8,128)S(1)}, f32[96,2048]{1,0:T(8,128)S(1)}, u32[]{:S(2)}, u32[]{:S(2)}) collective-permute-start(f32[96,2048]{1,0:T(8,128)S(1)} %get-tuple-element.32), channel_id=1, source_target_pairs={{0,4},{4,0},{8,12},{12,8},{16,20},{20,16},{24,28},{28,24},{32,36},... | collective-permute-start | bytes 2359304 | tf_op jit(solution)/shard_map/ppermute | solution.py:915
  12.8 34.5 %collective-permute-start.1 = (f32[96,2048]{1,0:T(8,128)S(1)}, f32[96,2048]{1,0:T(8,128)S(1)}, u32[]{:S(2)}, u32[]{:S(2)}) collective-permute-start(f32[96,2048]{1,0:T(8,128)S(1)} %get-tuple-element.33), channel_id=1, source_target_pairs={{0,124},{4,8},{8,4},{12,16},{16,12},{20,24},{24,20},{28,32},{32,28... | collective-permute-start | bytes 2359304 | tf_op jit(solution)/shard_map/ppermute | solution.py:916
  13.9 1.0 %copy-start.4 = (f32[16,2,2048]{2,1,0:T(2,128)S(1)}, f32[16,2,2048]{2,1,0:T(2,128)}, u32[]{:S(2)}) copy-start(f32[16,2,2048]{2,1,0:T(2,128)} %refs_10_.1) | copy-start | bytes 786436
  23.9 8.6 %copy-start.3 = (f32[16,2,2048]{2,1,0:T(2,128)S(1)}, f32[16,2,2048]{2,1,0:T(2,128)}, u32[]{:S(2)}) copy-start(f32[16,2,2048]{2,1,0:T(2,128)} %mark_ref.1) | copy-start | bytes 786436
  23.9 8.6 %copy-start.5 = (f32[16,2,2048]{2,1,0:T(2,128)S(1)}, f32[16,2,2048]{2,1,0:T(2,128)}, u32[]{:S(2)}) copy-start(f32[16,2,2048]{2,1,0:T(2,128)} %refs_10_.1) | copy-start | bytes 786436
  68.5 18.5 %copy-start.8 = (s32[16,2048]{1,0:T(8,128)S(1)}, s32[16,2048]{1,0:T(8,128)}, u32[]{:S(2)}) copy-start(s32[16,2048]{1,0:T(8,128)} %param.13) | copy-start | bytes 393220

commit v3 on v2

--- a/solution.py
+++ b/solution.py
@@ -807,12 +807,12 @@
                     out = out + grad_ref[row0 : row0 + SUBLANES, lanes]
                 grad_ref[row0 : row0 + SUBLANES, lanes] = out
 
-            def two_tiles(t, _, tile_step=tile_step):
-                tile_step(2 * t)
-                tile_step(2 * t + 1)
+            def four_tiles(t, _, tile_step=tile_step):
+                for n in range(4):
+                    tile_step(4 * t + n)
                 return 0
 
-            lax.fori_loop(0, tiles // 2, two_tiles, 0)
+            lax.fori_loop(0, tiles // 4, four_tiles, 0)
             at = pl.ds(group.start, SUBLANES), slice(None), pl.ds(row0, SUBLANES)
             for stage, hbm in ((fwd_stage, fwd_hbm), (adj_stage, adj_hbm)):
                 copies.append(pltpu.make_async_copy(stage.at[at], hbm.at[at], sems.at[len(copies)]))

time: 88.8 us -> 88.5 us (level); the launches traced: 87.7 us -> 88.5 us
  blocking collectives: 25.2 us -> 26.7 us
    all_gather x1, blocking collectives: 10 us -> 12.4 us  [local(): summed_terms = lax.all_gather(partial, 'wa').sum(axis=0)]
    all_to_all x1, blocking collectives: 15.2 us -> 14.3 us  [local(): lax.all_to_all(sums, 'gx', 0, 0, tiled=True)]
  transfers between devices with their start and end apart: 4 -> 4, of which waited for: 2 -> 2; matrix products, arithmetic and copies ran while one was open for 0% -> 0% of each run, Pallas kernels for 29% -> 28%
where the time goes in v3:
time: 88.5 us
  Pallas kernels  39.3 us (44%)
  blocking collectives  26.7 us (30%)
  starting transfers between devices  8.72 us (10%)
  waiting for transfers between devices  7.7 us (9%)
  local copies, waits for them, and re-layouts  4.46 us (5%)
    pallas_call x2, Pallas kernels, inner_rows(): pl.pallas_call(functools.partial(inner_kernel, forward=forward, total_row...  17.8 us
    all_to_all x1, blocking collectives, local(): lax.all_to_all(sums, 'gx', 0, 0, tiled=True)  14.3 us
    all_gather x1, blocking collectives, local(): summed_terms = lax.all_gather(partial, 'wa').sum(axis=0)  12.4 us
    pallas_call x2, Pallas kernels, outer_rows_solve(): pl.pallas_call(functools.partial(outer_kernel, forward=forward, total_row...  10.7 us
    pallas_call x1, Pallas kernels, finish(): pl.pallas_call(functools.partial(finish_kernel, total_rows=total_rows), i...  8.31 us
    ppermute x1, starting transfers between devices, local(): lax.ppermute(fwd_second, 'gx', pairing_two)  5.62 us
    ppermute x1, waiting for transfers between devices, local(): lax.ppermute(adj_second, 'gx', pairing_two)  5.54 us
    unnamed x26, local copies, waits for them, and re-layouts  4.42 us
  transfers between devices with their start and end apart: 4, of which 2 were waited for; matrix products, arithmetic and copies ran while one was open for 0% of the time, Pallas kernels for 28%

profile of v3, /device:TPU:1, one launch (start us, length us, event | category | flops | bytes accessed | tf_op | source)
XLA Modules:
  0.0 88.5 jit_solution(1863716174052666718)
XLA Ops:
  0.6 0.0 copy-start.10
  0.6 0.0 copy-start.9
  0.7 0.0 copy-start.12
  0.7 0.0 copy-start.11
  0.7 0.0 copy-start
  0.7 0.0 copy-start.1
  0.7 2.3 %copy-done.1 = f32[16,2,16,2048]{3,2,1,0:T(8,128)S(1)} copy-done((f32[16,2,16,2048]{3,2,1,0:T(8,128)S(1)}, f32[16,2,16,2048]{3,2,1,0:T(8,128)}, u32[]{:S(2)}) %copy-start.1) | copy-done | bytes 4194328
  3.0 0.0 copy-start.6
  3.0 1.1 %copy-done.6 = f32[16,2048]{1,0:T(8,128)S(1)} copy-done((f32[16,2048]{1,0:T(8,128)S(1)}, f32[16,2048]{1,0:T(8,128)}, u32[]{:S(2)}) %copy-start.6) | copy-done | bytes 131096
  4.1 0.0 copy-start.2
  4.1 0.0 copy-start.7
  4.1 0.4 outer_rows.3
  4.6 2.1 %collective-permute-start.2 = (f32[104,2048]{1,0:T(8,128)S(1)}, f32[104,2048]{1,0:T(8,128)S(1)}, u32[]{:S(2)}, u32[]{:S(2)}) collective-permute-start(f32[104,2048]{1,0:T(8,128)S(1)} %get-tuple-element.40), channel_id=1, source_target_pairs={{0,4},{4,0},{8,12},{12,8},{16,20},{20,16},{24,28},{28,24},{32,36},... | collective-permute-start | bytes 2555912 | tf_op jit(solution)/shard_map/ppermute | solution.py:910
  6.7 5.6 %collective-permute-start.3 = (f32[104,2048]{1,0:T(8,128)S(1)}, f32[104,2048]{1,0:T(8,128)S(1)}, u32[]{:S(2)}, u32[]{:S(2)}) collective-permute-start(f32[104,2048]{1,0:T(8,128)S(1)} %get-tuple-element.41), channel_id=1, source_target_pairs={{0,124},{4,8},{8,4},{12,16},{16,12},{20,24},{24,20},{28,32},{32,28... | collective-permute-start | bytes 2555912 | tf_op jit(solution)/shard_map/ppermute | solution.py:911
  12.3 0.0 copy-done
  12.3 0.4 outer_rows.2
  12.7 0.1 collective-permute-start
  12.8 0.9 %collective-permute-start.1 = (f32[96,2048]{1,0:T(8,128)S(1)}, f32[96,2048]{1,0:T(8,128)S(1)}, u32[]{:S(2)}, u32[]{:S(2)}) collective-permute-start(f32[96,2048]{1,0:T(8,128)S(1)} %get-tuple-element.33), channel_id=1, source_target_pairs={{0,124},{4,8},{8,4},{12,16},{16,12},{20,24},{24,20},{28,32},{32,28... | collective-permute-start | bytes 2359304 | tf_op jit(solution)/shard_map/ppermute | solution.py:916
  13.7 0.0 copy-done.10
  13.7 0.0 copy-done.9
  13.7 0.1 pad_add_fusion.refs_0_.whole_ref
  13.8 0.0 copy-done.12
  13.8 0.0 copy-done.11
  13.8 0.1 pad_maximum_fusion.refs_1_.real_ref
  13.9 0.0 copy-done.2
  13.9 0.0 copy-done.7
  13.9 0.0 copy-start.4
  13.9 0.9 %copy-done.4 = f32[16,2,2048]{2,1,0:T(2,128)S(1)} copy-done((f32[16,2,2048]{2,1,0:T(2,128)S(1)}, f32[16,2,2048]{2,1,0:T(2,128)}, u32[]{:S(2)}) %copy-start.4) | copy-done | bytes 262168
  14.9 9.3 %forward_inner.1 = (f32[22,2,16,2048]{3,2,1,0:T(8,128)S(1)}, f32[20,2,16,2048]{3,2,1,0:T(8,128)S(1)}, f32[18,2,16,2048]{3,2,1,0:T(8,128)S(1)}, f32[8,128]{1,0:T(...) custom-call(s32[33]{0:T(128)S(1)} %pad_add_fusion.refs_0_.whole_ref, ...), custom_call_target="tpu_custom_call" | custom-call | tf_op jit(solution)/shard_map/forward_inner/pallas_call | solution.py:646
  24.1 0.0 copy-start.3
  24.2 0.0 copy-start.5
  24.2 8.5 %adjoint_inner.1 = (f32[22,2,16,2048]{3,2,1,0:T(8,128)S(1)}, f32[20,2,16,2048]{3,2,1,0:T(8,128)S(1)}, f32[18,2,16,2048]{3,2,1,0:T(8,128)S(1)}, f32[8,128]{1,0:T(8,128)S(1)}) custom-call(s32[33]{0:T(128)S(1)} %pad_add_fusion.refs_0_.whole_ref, f32[48]{0:T(128)S(1)} %pad_maximum_fusion.refs_1_.real_ref, f32[16,2,16,2048]{3,2,1,0:T(8,128)S(1)} %copy-done, ...), custom_call_target="tpu_custom_call" | custom-call | tf_op jit(solution)/shard_map/adjoint_inner/pallas_call | solution.py:646
  32.7 0.0 collective-permute-done.2.refs_2_
  32.7 0.0 collective-permute-done.3.refs_3_
  32.7 0.0 copy-done.3
  32.7 0.0 copy-done.5
  32.7 5.2 %forward_outer.1 = (f32[22,2,16,2048]{3,2,1,0:T(8,128)S(1)}, f32[20,2,16,2048]{3,2,1,0:T(8,128)S(1)}, f32[18,2,16,2048]{3,2,1,0:T(8,128)S(1)}, f32[20,16,2048]{2...) custom-call(s32[33]{0:T(128)S(1)} %pad_add_fusion.refs_0_.whole_ref,, ...), custom_call_target="tpu_custom_call", output_to_operand_aliasing={{0}: (5, {}), {1}: (6, {}), {2}: (7, {}), {3}: (8, {}), {4}... | custom-call | tf_op jit(solution)/shard_map/forward_outer/pallas_call | solution.py:674
  37.9 1.7 %adjoint_line.1 = (f32[6,2,16,2048]{3,2,1,0:T(8,128)S(1)}, f32[27,16,128]{2,1,0:T(8,128)S(1)}) custom-call(s32[33]{0:T(128)S(1)} %pad_add_fusion.refs_0_.whole_ref, f32[48]{0:T(128)S(1)} %pad_maximum_fusion.refs_1_.real_ref, f32[20,2,16,2048]{3,2,1,0:T(8,128)S(1)} %get-tuple-element.38.z_ref.refs_6_, ...), custom_call_target="tpu_custom_call" | custom-call | tf_op jit(solution)/shard_map/adjoint_line/pallas_call | solution.py:620
  39.6 2.2 %collective-permute-done.refs_2_ = f32[96,2048]{1,0:T(8,128)S(1)} collective-permute-done((f32[96,2048]{1,0:T(8,128)S(1)}, f32[96,2048]{1,0:T(8,128)S(1)}, u32[]{:S(2)}, u32[]{:S(2)}) %collective-permute-start) | collective-permute-done | bytes 786464 | tf_op jit(solution)/shard_map/ppermute | solution.py:915
  41.8 5.5 %collective-permute-done.1.refs_3_ = f32[96,2048]{1,0:T(8,128)S(1)} collective-permute-done((f32[96,2048]{1,0:T(8,128)S(1)}, f32[96,2048]{1,0:T(8,128)S(1)}, u32[]{:S(2)}, u32[]{:S(2)}) %collective-permute-start.1) | collective-permute-done | bytes 786464 | tf_op jit(solution)/shard_map/ppermute | solution.py:916
  47.3 5.5 %adjoint_outer.1 = (f32[22,2,16,2048]{3,2,1,0:T(8,128)S(1)}, f32[20,2,16,2048]{3,2,1,0:T(8,128)S(1)}, f32[18,2,16,2048]{3,2,1,0:T(8,128)S(1)}, f32[32,8,128]{2,1,0:T(8,128)S(1)}) custom-call(s32[33]{0:T(128)S(1)} %pad_add_fusion.refs_0_.whole_ref, ...), custom_call_target="tpu_custom_call", output_to_operand_aliasing={{0}: (5, {}), {1}: (6, {}), {2}: (7, {})} | custom-call | tf_op jit(solution)/shard_map/adjoint_outer/pallas_call | solution.py:674
  52.8 14.3 %all_to_all.5.sums_ref = f32[32,8,128]{2,1,0:T(8,128)S(1)} all-to-all(f32[32,8,128]{2,1,0:T(8,128)S(1)} %get-tuple-element.51), channel_id=1, replica_groups=mesh['gx'=32,'wa'=4] {'gx'}, dimensions={0} | all-to-all | bytes 262144 | tf_op jit(solution)/shard_map/all_to_all | solution.py:947
  67.1 0.0 copy-start.8
  67.1 8.3 %finish.1 = (f32[16,2,16,2048]{3,2,1,0:T(8,128)}, f32[16,2,16,2048]{3,2,1,0:T(8,128)}, f32[16,2048]{1,0:T(8,128)S(1)}, f32[20,2,16,2048]{3,2,1,0:T(8,128)S(1)}, f32[18,2,16,2048]{3,2,1,0:T(8,128)S(1)}) custom-call(s32[33]{0:T(128)S(1)} %pad_add_fusion.refs_0_.whole_ref, ...), custom_call_target="tpu_custom_call", output_to_operand_aliasing={{3}: (7, {}), {4}: (8, {})} | custom-call | tf_op jit(solution)/shard_map/finish/pallas_call | solution.py:829
  75.4 12.4 %all-gather = f32[64,2048]{1,0:T(8,128)S(1)} all-gather(f32[16,2048]{1,0:T(8,128)S(1)} %get-tuple-element.60), channel_id=2, replica_groups=mesh['gx'=32,'wa'=4] {'wa'}, dimensions={0}, use_global_device_ids=true | all-gather | bytes 655360 | tf_op jit(solution)/shard_map/all_gather | solution.py:953
  87.9 0.0 copy-done.8
  87.9 0.7 convert_multiply_fusion
  (2 shorter events, 0.1 us)
Async XLA Ops:
  0.6 13.1 %copy-start.10 = (s32[16]{0:T(128)S(1)}, s32[16]{0:T(128)}, u32[]{:S(2)}) copy-start(s32[16]{0:T(128)} %param.14) | copy-start | bytes 196
  0.6 13.1 %copy-start.9 = (s32[16]{0:T(128)S(1)}, s32[16]{0:T(128)}, u32[]{:S(2)}) copy-start(s32[16]{0:T(128)} %param.15) | copy-start | bytes 196
  0.7 13.1 %copy-start.12 = (f32[16]{0:T(128)S(1)}, f32[16]{0:T(128)}, u32[]{:S(2)}) copy-start(f32[16]{0:T(128)} %param.17) | copy-start | bytes 196
  0.7 13.2 %copy-start.11 = (f32[16]{0:T(128)S(1)}, f32[16]{0:T(128)}, u32[]{:S(2)}) copy-start(f32[16]{0:T(128)} %param.16) | copy-start | bytes 196
  0.7 11.6 %copy-start = (f32[16,2,16,2048]{3,2,1,0:T(8,128)S(1)}, f32[16,2,16,2048]{3,2,1,0:T(8,128)}, u32[]{:S(2)}) copy-start(f32[16,2,16,2048]{3,2,1,0:T(8,128)} %refs_2_.3) | copy-start | bytes 12582916
  0.7 2.3 %copy-start.1 = (f32[16,2,16,2048]{3,2,1,0:T(8,128)S(1)}, f32[16,2,16,2048]{3,2,1,0:T(8,128)}, u32[]{:S(2)}) copy-start(f32[16,2,16,2048]{3,2,1,0:T(8,128)} %field_ref.3) | copy-start | bytes 12582916
  3.0 1.1 %copy-start.6 = (f32[16,2048]{1,0:T(8,128)S(1)}, f32[16,2048]{1,0:T(8,128)}, u32[]{:S(2)}) copy-start(f32[16,2048]{1,0:T(8,128)} %refs_0_.1) | copy-start | bytes 393220
  4.1 9.8 %copy-start.2 = (f32[16,2,16,2048]{3,2,1,0:T(8,128)S(1)}, f32[16,2,16,2048]{3,2,1,0:T(8,128)}, u32[]{:S(2)}) copy-start(f32[16,2,16,2048]{3,2,1,0:T(8,128)} %field_ref.3) | copy-start | bytes 12582916
  4.1 9.8 %copy-start.7 = (f32[16,2048]{1,0:T(8,128)S(1)}, f32[16,2048]{1,0:T(8,128)}, u32[]{:S(2)}) copy-start(f32[16,2048]{1,0:T(8,128)} %refs_0_.1) | copy-start | bytes 393220
  4.6 28.1 %collective-permute-start.2 = (f32[104,2048]{1,0:T(8,128)S(1)}, f32[104,2048]{1,0:T(8,128)S(1)}, u32[]{:S(2)}, u32[]{:S(2)}) collective-permute-start(f32[104,2048]{1,0:T(8,128)S(1)} %get-tuple-element.40), channel_id=1, source_target_pairs={{0,4},{4,0},{8,12},{12,8},{16,20},{20,16},{24,28},{28,24},{32,36},... | collective-permute-start | bytes 2555912 | tf_op jit(solution)/shard_map/ppermute | solution.py:910
  6.7 26.0 %collective-permute-start.3 = (f32[104,2048]{1,0:T(8,128)S(1)}, f32[104,2048]{1,0:T(8,128)S(1)}, u32[]{:S(2)}, u32[]{:S(2)}) collective-permute-start(f32[104,2048]{1,0:T(8,128)S(1)} %get-tuple-element.41), channel_id=1, source_target_pairs={{0,124},{4,8},{8,4},{12,16},{16,12},{20,24},{24,20},{28,32},{32,28... | collective-permute-start | bytes 2555912 | tf_op jit(solution)/shard_map/ppermute | solution.py:911
  12.7 29.1 %collective-permute-start = (f32[96,2048]{1,0:T(8,128)S(1)}, f32[96,2048]{1,0:T(8,128)S(1)}, u32[]{:S(2)}, u32[]{:S(2)}) collective-permute-start(f32[96,2048]{1,0:T(8,128)S(1)} %get-tuple-element.32), channel_id=1, source_target_pairs={{0,4},{4,0},{8,12},{12,8},{16,20},{20,16},{24,28},{28,24},{32,36},... | collective-permute-start | bytes 2359304 | tf_op jit(solution)/shard_map/ppermute | solution.py:915
  12.8 34.5 %collective-permute-start.1 = (f32[96,2048]{1,0:T(8,128)S(1)}, f32[96,2048]{1,0:T(8,128)S(1)}, u32[]{:S(2)}, u32[]{:S(2)}) collective-permute-start(f32[96,2048]{1,0:T(8,128)S(1)} %get-tuple-element.33), channel_id=1, source_target_pairs={{0,124},{4,8},{8,4},{12,16},{16,12},{20,24},{24,20},{28,32},{32,28... | collective-permute-start | bytes 2359304 | tf_op jit(solution)/shard_map/ppermute | solution.py:916
  13.9 1.0 %copy-start.4 = (f32[16,2,2048]{2,1,0:T(2,128)S(1)}, f32[16,2,2048]{2,1,0:T(2,128)}, u32[]{:S(2)}) copy-start(f32[16,2,2048]{2,1,0:T(2,128)} %refs_10_.1) | copy-start | bytes 786436
  24.1 8.6 %copy-start.3 = (f32[16,2,2048]{2,1,0:T(2,128)S(1)}, f32[16,2,2048]{2,1,0:T(2,128)}, u32[]{:S(2)}) copy-start(f32[16,2,2048]{2,1,0:T(2,128)} %mark_ref.1) | copy-start | bytes 786436
  24.2 8.6 %copy-start.5 = (f32[16,2,2048]{2,1,0:T(2,128)S(1)}, f32[16,2,2048]{2,1,0:T(2,128)}, u32[]{:S(2)}) copy-start(f32[16,2,2048]{2,1,0:T(2,128)} %refs_10_.1) | copy-start | bytes 786436
  67.1 20.7 %copy-start.8 = (s32[16,2048]{1,0:T(8,128)S(1)}, s32[16,2048]{1,0:T(8,128)}, u32[]{:S(2)}) copy-start(s32[16,2048]{1,0:T(8,128)} %param.13) | copy-start | bytes 393220
